TPU v7x, 32 devices: a whole 2x2x4 slice. The times are simulated.
32 devices in a mesh: dp: 2 (over x), col: 4 (over z), row: 4 (over y, core).
Axes of the slice: x: 2, y: 2, z: 4, core: 2. Of those that a mesh axis runs over, the one named last changes fastest.
Arguments:
- left_mat: bfloat16 [65536, 2048], P(('dp', 'row'), 'col'), parts along dimension 0
- right_mat: bfloat16 [2048, 8192], P('row', 'col')
Outputs:
- output: bfloat16 [65536, 8192], P(('dp', 'row'), 'col'), parts along dimension 0
There are 2 independent parts. A program takes and returns all parts, laid end to end along the dimension named above; an argument that names none is the same for every part.
All inputs are finite; a program needn't handle non-finite values.
Results may differ from a plain program's by a relative error of at most 0.001.
Values are sent between devices in bfloat16 or wider.
A program may use at most 1 GiB of HBM per device.

v0:
```python
import jax
import jax.numpy as jnp
from jax import lax
from jax.sharding import PartitionSpec as P


def solution(mesh):
    grid_side = mesh.shape["row"]
    skew_left = [(((row_pos + col_pos) % grid_side) * grid_side + row_pos, col_pos * grid_side + row_pos) for row_pos in range(grid_side) for col_pos in range(grid_side)]
    skew_right = [(col_pos * grid_side + (row_pos + col_pos) % grid_side, col_pos * grid_side + row_pos) for row_pos in range(grid_side) for col_pos in range(grid_side)]
    shift_pairs = [((pos_idx + 1) % grid_side, pos_idx) for pos_idx in range(grid_side)]

    def cannon_local(left_blk, right_blk):
        left_cur = lax.ppermute(left_blk, ("col", "row"), skew_left)
        right_cur = lax.ppermute(right_blk, ("col", "row"), skew_right)
        acc_sum = jnp.dot(left_cur, right_cur, preferred_element_type=jnp.float32)
        for step_num in range(1, grid_side):
            left_cur = lax.ppermute(left_cur, "col", shift_pairs)
            right_cur = lax.ppermute(right_cur, "row", shift_pairs)
            acc_sum = acc_sum + jnp.dot(left_cur, right_cur, preferred_element_type=jnp.float32)
        return acc_sum.astype(jnp.bfloat16)

    return jax.shard_map(cannon_local, mesh=mesh, in_specs=(P(("dp", "row"), "col"), P("row", "col")), out_specs=P(("dp", "row"), "col"), check_vma=False)
```

profile of v0, /device:TPU:28, one launch (start us, length us, event | category | flops | bytes accessed | tf_op | source)
XLA Modules:
  0.0 981.2 jit_solution(5951562078536161834)
XLA Ops:
  0.0 2.2 collective-permute-start
  2.2 361.5 %collective-permute-done = bf16[8192,512]{1,0:T(8,128)(2,1)S(1)} collective-permute-done((bf16[8192,512]{1,0:T(8,128)(2,1)}, bf16[8192,512]{1,0:T(8,128)(2,1)S(1)}, u32[]{:S(2)}, u32[]{:S(2)}) %collective-permute-start) | collective-permute-done | bytes 8388640 | tf_op jit(solution)/shard_map/ppermute | solution.py:14
  363.7 0.0 copy-start
  363.7 0.0 collective-permute-start.2
  363.7 178.0 %collective-permute-done.2 = bf16[8192,512]{1,0:T(8,128)(2,1)} collective-permute-done((bf16[8192,512]{1,0:T(8,128)(2,1)S(1)}, bf16[8192,512]{1,0:T(8,128)(2,1)}, u32[]{:S(2)}, u32[]{:S(2)}) %collective-permute-start.2) | collective-permute-done | bytes 8388640 | tf_op jit(solution)/shard_map/ppermute | solution.py:18
  541.7 2.5 collective-permute-start.4
  544.2 1.9 collective-permute-start.1
  546.2 27.5 %collective-permute-done.1 = bf16[512,2048]{1,0:T(8,128)(2,1)} collective-permute-done((bf16[512,2048]{1,0:T(8,128)(2,1)}, bf16[512,2048]{1,0:T(8,128)(2,1)}, u32[]{:S(2)}, u32[]{:S(2)}) %collective-permute-start.1) | collective-permute-done | bytes 2097184 | tf_op jit(solution)/shard_map/ppermute | solution.py:15
  573.6 0.0 collective-permute-start.3
  573.6 23.5 %collective-permute-done.3 = bf16[512,2048]{1,0:T(8,128)(2,1)} collective-permute-done((bf16[512,2048]{1,0:T(8,128)(2,1)}, bf16[512,2048]{1,0:T(8,128)(2,1)}, u32[]{:S(2)}, u32[]{:S(2)}) %collective-permute-start.3) | collective-permute-done | bytes 2097184 | tf_op jit(solution)/shard_map/ppermute | solution.py:19
  597.2 1.9 collective-permute-start.5
  599.1 0.0 copy-done
  599.1 23.5 %collective-permute-done.5 = bf16[512,2048]{1,0:T(8,128)(2,1)} collective-permute-done((bf16[512,2048]{1,0:T(8,128)(2,1)}, bf16[512,2048]{1,0:T(8,128)(2,1)}, u32[]{:S(2)}, u32[]{:S(2)}) %collective-permute-start.5) | collective-permute-done | bytes 2097184 | tf_op jit(solution)/shard_map/ppermute | solution.py:19
  622.6 1.9 collective-permute-start.7
  624.6 98.6 %collective-permute-done.4 = bf16[8192,512]{1,0:T(8,128)(2,1)} collective-permute-done((bf16[8192,512]{1,0:T(8,128)(2,1)}, bf16[8192,512]{1,0:T(8,128)(2,1)}, u32[]{:S(2)}, u32[]{:S(2)}) %collective-permute-start.4) | collective-permute-done | bytes 8388640 | tf_op jit(solution)/shard_map/ppermute | solution.py:18
  723.2 1.6 collective-permute-start.6
  724.8 30.9 %fusion = f32[8192,2048]{1,0:T(8,128)} fusion(bf16[8192,512]{1,0:T(8,128)(2,1)} %copy-done, bf16[512,2048]{1,0:T(8,128)(2,1)} %collective-permute-done.1), kind=kOutput, calls=%fused_computation.1 | convolution fusion | flops 17179869184 | bytes 77594624 | tf_op jit(solution)/shard_map/dot_general | solution.py:16
  755.7 30.9 %fusion.1 = f32[8192,2048]{1,0:T(8,128)} fusion(bf16[8192,512]{1,0:T(8,128)(2,1)} %collective-permute-done.2, bf16[512,2048]{1,0:T(8,128)(2,1)} %collective-permute-done.3), kind=kOutput, calls=%fused_computation.2 | convolution fusion | flops 17179869184 | bytes 77594624 | tf_op jit(solution)/shard_map/dot_general | solution.py:20
  786.6 30.9 %fusion.2 = f32[8192,2048]{1,0:T(8,128)} fusion(bf16[8192,512]{1,0:T(8,128)(2,1)} %collective-permute-done.4, bf16[512,2048]{1,0:T(8,128)(2,1)} %collective-permute-done.5), kind=kOutput, calls=%fused_computation.3 | convolution fusion | flops 17179869184 | bytes 77594624 | tf_op jit(solution)/shard_map/dot_general | solution.py:20
  817.5 0.0 collective-permute-done.7
  817.5 86.0 %collective-permute-done.6 = bf16[8192,512]{1,0:T(8,128)(2,1)} collective-permute-done((bf16[8192,512]{1,0:T(8,128)(2,1)}, bf16[8192,512]{1,0:T(8,128)(2,1)}, u32[]{:S(2)}, u32[]{:S(2)}) %collective-permute-start.6) | collective-permute-done | bytes 8388640 | tf_op jit(solution)/shard_map/ppermute | solution.py:18
  903.6 77.7 %add_convert_fusion = bf16[8192,2048]{1,0:T(8,128)(2,1)} fusion(f32[8192,2048]{1,0:T(8,128)} %fusion.2, f32[8192,2048]{1,0:T(8,128)} %fusion, f32[8192,2048]{1,0:T(8,128)} %fusion.1, bf16[8192,512]{1,0:T(8,128)(2,1)} %collective-permute-done.6, bf16[512,2048]{1,0:T(8,128)(2,1)S(1)} %collective-permute-done.7), kind=kOutput, calls=%fused_computation | convolution fusion | flops 17246978048 | bytes 245366784 | tf_op jit(solution)/shard_map/dot_general | solution.py:20
Async XLA Ops:
  0.0 363.7 %collective-permute-start = (bf16[8192,512]{1,0:T(8,128)(2,1)}, bf16[8192,512]{1,0:T(8,128)(2,1)S(1)}, u32[]{:S(2)}, u32[]{:S(2)}) collective-permute-start(bf16[8192,512]{1,0:T(8,128)(2,1)} %param.2), channel_id=1, source_target_pairs={{0,0},{4,4},{8,8},{12,12},{5,1},{9,5},{13,9},{1,13},{10,2},{14,6},... | collective-permute-start | bytes 25165832 | tf_op jit(solution)/shard_map/ppermute | solution.py:14
  363.7 235.4 %copy-start = (bf16[8192,512]{1,0:T(8,128)(2,1)}, bf16[8192,512]{1,0:T(8,128)(2,1)S(1)}, u32[]{:S(2)}) copy-start(bf16[8192,512]{1,0:T(8,128)(2,1)S(1)} %collective-permute-done) | copy-start | bytes 25165828
  363.7 178.0 %collective-permute-start.2 = (bf16[8192,512]{1,0:T(8,128)(2,1)S(1)}, bf16[8192,512]{1,0:T(8,128)(2,1)}, u32[]{:S(2)}, u32[]{:S(2)}) collective-permute-start(bf16[8192,512]{1,0:T(8,128)(2,1)S(1)} %collective-permute-done), channel_id=1, source_target_pairs={{4,0},{8,4},{12,8},{0,12},{5,1},{9,5},{13,9},{1,13},{6,2},{10,6},{... | collective-permute-start | bytes 25165832 | tf_op jit(solution)/shard_map/ppermute | solution.py:18
  541.7 181.4 %collective-permute-start.4 = (bf16[8192,512]{1,0:T(8,128)(2,1)}, bf16[8192,512]{1,0:T(8,128)(2,1)}, u32[]{:S(2)}, u32[]{:S(2)}) collective-permute-start(bf16[8192,512]{1,0:T(8,128)(2,1)} %collective-permute-done.2), channel_id=1, source_target_pairs={{4,0},{8,4},{12,8},{0,12},{5,1},{9,5},{13,9},{1,13},{6,2},{10,6},{... | collective-permute-start | bytes 25165832 | tf_op jit(solution)/shard_map/ppermute | solution.py:18
  544.2 29.4 %collective-permute-start.1 = (bf16[512,2048]{1,0:T(8,128)(2,1)}, bf16[512,2048]{1,0:T(8,128)(2,1)}, u32[]{:S(2)}, u32[]{:S(2)}) collective-permute-start(bf16[512,2048]{1,0:T(8,128)(2,1)} %param.3), channel_id=1, source_target_pairs={{0,0},{5,4},{10,8},{15,12},{1,1},{6,5},{11,9},{12,13},{2,2},{7,6},... | collective-permute-start | bytes 6291464 | tf_op jit(solution)/shard_map/ppermute | solution.py:15
  573.6 23.5 %collective-permute-start.3 = (bf16[512,2048]{1,0:T(8,128)(2,1)}, bf16[512,2048]{1,0:T(8,128)(2,1)}, u32[]{:S(2)}, u32[]{:S(2)}) collective-permute-start(bf16[512,2048]{1,0:T(8,128)(2,1)} %collective-permute-done.1), channel_id=1, source_target_pairs={{1,0},{2,1},{3,2},{0,3},{5,4},{6,5},{7,6},{4,7},{9,8},{10,9},{11,1... | collective-permute-start | bytes 6291464 | tf_op jit(solution)/shard_map/ppermute | solution.py:19
  597.2 25.5 %collective-permute-start.5 = (bf16[512,2048]{1,0:T(8,128)(2,1)}, bf16[512,2048]{1,0:T(8,128)(2,1)}, u32[]{:S(2)}, u32[]{:S(2)}) collective-permute-start(bf16[512,2048]{1,0:T(8,128)(2,1)} %collective-permute-done.3), channel_id=1, source_target_pairs={{1,0},{2,1},{3,2},{0,3},{5,4},{6,5},{7,6},{4,7},{9,8},{10,9},{11,1... | collective-permute-start | bytes 6291464 | tf_op jit(solution)/shard_map/ppermute | solution.py:19
  622.6 194.9 %collective-permute-start.7 = (bf16[512,2048]{1,0:T(8,128)(2,1)}, bf16[512,2048]{1,0:T(8,128)(2,1)S(1)}, u32[]{:S(2)}, u32[]{:S(2)}) collective-permute-start(bf16[512,2048]{1,0:T(8,128)(2,1)} %collective-permute-done.5), channel_id=1, source_target_pairs={{1,0},{2,1},{3,2},{0,3},{5,4},{6,5},{7,6},{4,7},{9,8},{10,9},{11,1... | collective-permute-start | bytes 6291464 | tf_op jit(solution)/shard_map/ppermute | solution.py:19
  723.2 180.4 %collective-permute-start.6 = (bf16[8192,512]{1,0:T(8,128)(2,1)}, bf16[8192,512]{1,0:T(8,128)(2,1)}, u32[]{:S(2)}, u32[]{:S(2)}) collective-permute-start(bf16[8192,512]{1,0:T(8,128)(2,1)} %collective-permute-done.4), channel_id=1, source_target_pairs={{4,0},{8,4},{12,8},{0,12},{5,1},{9,5},{13,9},{1,13},{6,2},{10,6},{... | collective-permute-start | bytes 25165832 | tf_op jit(solution)/shard_map/ppermute | solution.py:18
where the time goes:
time: 983 us; the launch traced here: 981 us
  waiting for transfers between devices  799 us (81%)
  matrix products  170 us (17%)
  starting transfers between devices  12.1 us (1%)
    ppermute x3, waiting for transfers between devices, cannon_local(): left_cur = lax.ppermute(left_cur, 'col', shift_pairs)  363 us
    ppermute x1, waiting for transfers between devices, cannon_local(): left_cur = lax.ppermute(left_blk, ('col', 'row'), skew_left)  361 us
    dot_general x3, matrix products, cannon_local(): jnp.dot(left_cur, right_cur, preferred_element_type=jnp.float32)  139 us
    ppermute x3, waiting for transfers between devices, cannon_local(): right_cur = lax.ppermute(right_cur, 'row', shift_pairs)  47.1 us
    dot_general x1, matrix products, cannon_local(): acc_sum = jnp.dot(left_cur, right_cur, preferred_element_type=jnp.float32)  30.9 us
    ppermute x1, waiting for transfers between devices, cannon_local(): right_cur = lax.ppermute(right_blk, ('col', 'row'), skew_right)  27.5 us
  transfers between devices with their start and end apart: 8, of which 7 were waited for; matrix products, arithmetic and copies ran while one was open for 9% of the time, Pallas kernels for 0%

commit v1 on v0

v1 whole, which is shorter than its diff:
```python
import functools

import jax
import jax.numpy as jnp
from jax import lax
from jax.experimental import pallas as pl
from jax.experimental.pallas import tpu as pltpu
from jax.sharding import PartitionSpec as P


GROUPS = (1536, 1152, 768, 384, 256)
BM = 128


def _mm_kernel(steps, own_p, left_p, opp_p, right_p, own_m, left_m, opp_m, right_m, b_ref, *rest):
    out_ref = rest[-1]
    step = pl.program_id(0)

    def product(own, right, opp, left):
        lhs = jnp.concatenate([own[...], right[...], opp[...], left[...]], axis=1)
        out_ref[...] = jnp.dot(lhs, b_ref[...], preferred_element_type=jnp.float32).astype(out_ref.dtype)

    @pl.when(step < steps)
    def _():
        product(own_p, right_p, opp_p, left_p)

    @pl.when(step >= steps)
    def _():
        product(own_m, right_m, opp_m, left_m)


def _group_product(a, left_p, opp_p, right_p, left_m, opp_m, right_m, b, c, rows, cols, off, size, half):
    bm = min(BM, size)
    steps = size // bm
    depth = a.shape[1]
    total = depth * 4
    first = lambda i: jnp.minimum(i, steps - 1)
    second = lambda i: jnp.maximum(i - steps, 0)
    piece_p = pl.BlockSpec((bm, depth), lambda i: (first(i), 0))
    piece_m = pl.BlockSpec((bm, depth), lambda i: (second(i), 0))
    own_p = pl.BlockSpec((bm, depth), lambda i: (off // bm + first(i), 0))
    own_m = pl.BlockSpec((bm, depth), lambda i: ((half + off) // bm + second(i), 0))
    whole = pl.BlockSpec((total, cols), lambda i: (0, 0), pipeline_mode=pl.Buffered(1))
    out = pl.BlockSpec((bm, cols), lambda i: (jnp.where(i < steps, off // bm + i, (half + off) // bm + i - steps), 0))
    in_specs = [own_p, piece_p, piece_p, piece_p, own_m, piece_m, piece_m, piece_m, whole]
    args = [a, left_p, opp_p, right_p, a, left_m, opp_m, right_m, b]
    alias = {}
    if c is not None:
        in_specs.append(pl.BlockSpec(memory_space=pl.ANY))
        args.append(c)
        alias = {9: 0}
    return pl.pallas_call(
        functools.partial(_mm_kernel, steps),
        grid=(2 * steps,),
        out_shape=jax.ShapeDtypeStruct((rows, cols), jnp.bfloat16),
        in_specs=in_specs,
        out_specs=out,
        input_output_aliases=alias,
        compiler_params=pltpu.CompilerParams(dimension_semantics=("arbitrary",), vmem_limit_bytes=40 * 2**20),
        cost_estimate=pl.CostEstimate(
            flops=2 * 2 * size * total * cols,
            bytes_accessed=2 * size * (total + cols) * 2,
            transcendentals=0,
        ),
        name="group_product",
    )(*args)


def solution(mesh):
    side = mesh.shape["row"]
    up = [(p, (p + 1) % side) for p in range(side)]
    down = [(p, (p - 1) % side) for p in range(side)]

    def local(a, b_own):
        rows, depth = a.shape
        cols = b_own.shape[1]
        half = rows // 2
        offs = [sum(GROUPS[:g]) for g in range(len(GROUPS))]
        row_pos, col_pos = lax.axis_index("row"), lax.axis_index("col")

        a_p = [lax.slice_in_dim(a, o, o + s) for o, s in zip(offs, GROUPS)]
        a_m = [lax.slice_in_dim(a, half + o, half + o + s) for o, s in zip(offs, GROUPS)]
        left_p = [lax.ppermute(x, "col", up) for x in a_p]
        right_m = [lax.ppermute(x, "col", down) for x in a_m]

        b_all = [b_own] + [
            lax.ppermute(b_own, "row", [(p, (p - s) % side) for p in range(side)]) for s in range(1, side)
        ]
        b_twice = jnp.concatenate(b_all + b_all, axis=0)
        b = lax.dynamic_slice_in_dim(b_twice, lax.rem(col_pos - row_pos + side, side) * depth, side * depth)

        c = None
        for g, (off, size) in enumerate(zip(offs, GROUPS)):
            opp_p = lax.ppermute(left_p[g], "col", up)
            opp_m = lax.ppermute(right_m[g], "col", down)
            left_m = lax.ppermute(a_m[g], "col", up)
            right_p = lax.ppermute(a_p[g], "col", down)
            c = _group_product(
                a, left_p[g], opp_p, right_p, left_m, opp_m, right_m[g], b, c, rows, cols, off, size, half
            )
        return c

    return jax.shard_map(
        local, mesh=mesh, in_specs=(P(("dp", "row"), "col"), P("row", "col")),
        out_specs=P(("dp", "row"), "col"), check_vma=False,
    )
```

time: 983 us -> 573 us (0.58)
  waiting for transfers between devices: 799 us -> 385 us
  matrix products: 170 us -> 0 us
  Pallas kernels: 0 us -> 106 us
  local copies, waits for them, and re-layouts: 0.01 us -> 44 us
  starting transfers between devices: 12.1 us -> 35.5 us
    ppermute x8 -> x33, waiting for transfers between devices: 799 us -> 385 us  [the longest x5 185 us: local(): right_m = [lax.ppermute(x, 'col', down) for x in a_m]]
    dot_general x4 -> x0, matrix products: 170 us -> none  [the longest x3 139 us: cannon_local(): jnp.dot(left_cur, right_cur, preferred_element_type=jnp.float32)]
    pallas_call x0 -> x5, Pallas kernels: none -> 106 us  [_group_product(): pl.pallas_call(functools.partial(_mm_kernel, steps), grid=(2 * steps,), o...]
    ppermute x8 -> x33, starting transfers between devices: 12.1 us -> 35.5 us  [the longest x5 18.5 us: local(): left_m = lax.ppermute(a_m[g], 'col', up)]
    unnamed x2 -> x29, local copies, waits for them, and re-layouts: 0.01 us -> 20.4 us
    slice x0 -> x5, local copies, waits for them, and re-layouts: none -> 12 us  [local(): lax.slice_in_dim(a, half + o, half + o + s)]
  transfers between devices with their start and end apart: 8 -> 33, of which waited for: 7 -> 15; matrix products, arithmetic and copies ran while one was open for 9% -> 8% of each run, Pallas kernels for 0% -> 17%
where the time goes in v1:
time: 573 us; the launch traced here: 570 us
  waiting for transfers between devices  385 us (67%)
  Pallas kernels  106 us (18%)
  local copies, waits for them, and re-layouts  44 us (8%)
  starting transfers between devices  35.5 us (6%)
    ppermute x5, waiting for transfers between devices, local(): right_m = [lax.ppermute(x, 'col', down) for x in a_m]  185 us
    pallas_call x5, Pallas kernels, _group_product(): pl.pallas_call(functools.partial(_mm_kernel, steps), grid=(2 * steps,), o...  106 us
    ppermute x5, waiting for transfers between devices, local(): left_p = [lax.ppermute(x, 'col', up) for x in a_p]  65.7 us
    ppermute x5, waiting for transfers between devices, local(): opp_m = lax.ppermute(right_m[g], 'col', down)  59.6 us
    ppermute x5, waiting for transfers between devices, local(): opp_p = lax.ppermute(left_p[g], 'col', up)  37.3 us
    ppermute x3, waiting for transfers between devices, local(): lax.ppermute(b_own, 'row', [(p, (p - s) % side) for p in range(side)])  37.3 us
    unnamed x29, local copies, waits for them, and re-layouts  20.4 us
    ppermute x5, starting transfers between devices, local(): left_m = lax.ppermute(a_m[g], 'col', up)  18.5 us
  transfers between devices with their start and end apart: 33, of which 15 were waited for; matrix products, arithmetic and copies ran while one was open for 8% of the time, Pallas kernels for 17%

profile of v1, /device:TPU:28, one launch (start us, length us, event | category | flops | bytes accessed | tf_op | source)
XLA Modules:
  0.0 570.5 jit_solution(16605707785127552923)
XLA Ops:
  0.0 1.5 collective-permute-start.7
  1.5 3.7 fusion
  5.4 1.8 fusion.4
  7.2 1.6 collective-permute-start
  8.7 2.7 fusion.2
  11.4 3.2 constant_dynamic-update-slice_fusion.7
  14.5 33.4 %collective-permute-done.left_p = bf16[256,512]{1,0:T(8,128)(2,1)S(1)} collective-permute-done((bf16[256,512]{1,0:T(8,128)(2,1)S(1)}, bf16[256,512]{1,0:T(8,128)(2,1)S(1)}, u32[]{:S(2)}, u32[]{:S(2)}) %collective-permute-start) | collective-permute-done | bytes 262176 | tf_op jit(solution)/shard_map/ppermute | solution.py:83
  48.4 1.9 fusion.3
  50.4 2.0 fusion.1
  52.4 3.4 collective-permute-start.21
  55.8 37.3 %collective-permute-done.7 = bf16[512,2048]{1,0:T(8,128)(2,1)} collective-permute-done((bf16[512,2048]{1,0:T(8,128)(2,1)}, bf16[512,2048]{1,0:T(8,128)(2,1)}, u32[]{:S(2)}, u32[]{:S(2)}) %collective-permute-start.7) | collective-permute-done | bytes 2097184 | tf_op jit(solution)/shard_map/ppermute | solution.py:87
  93.3 3.2 constant_dynamic-update-slice_fusion.6
  96.5 1.6 collective-permute-start.9
  98.1 3.2 constant_dynamic-update-slice_fusion.5
  101.2 3.2 constant_dynamic-update-slice_fusion.4
  104.4 32.3 %collective-permute-done.9.left_p = bf16[384,512]{1,0:T(8,128)(2,1)S(1)} collective-permute-done((bf16[384,512]{1,0:T(8,128)(2,1)S(1)}, bf16[384,512]{1,0:T(8,128)(2,1)S(1)}, u32[]{:S(2)}, u32[]{:S(2)}) %collective-permute-start.9) | collective-permute-done | bytes 393248 | tf_op jit(solution)/shard_map/ppermute | solution.py:83
  136.7 0.6 collective-permute-start.29
  137.2 3.3 collective-permute-start.30
  140.6 2.0 collective-permute-start.32
  142.5 1.5 constant_dynamic-update-slice_fusion.3
  144.0 3.2 constant_dynamic-update-slice_fusion.2
  147.2 3.2 constant_dynamic-update-slice_fusion.1
  150.3 3.2 constant_dynamic-update-slice_fusion
  153.5 8.3 %constant_dynamic-slice_fusion.b_ref = bf16[2048,2048]{1,0:T(8,128)(2,1)} fusion(bf16[4096,2048]{1,0:T(8,128)(2,1)} %constant_dynamic-update-slice_fusion, s32[]{:T(128)S(6)} %select_n.3), kind=kLoop, calls=%fused_computation.8 | loop fusion | bytes 16777220 | tf_op jit(solution)/shard_map/dynamic_slice | solution.py:90
  161.8 139.6 %collective-permute-done.25.right_m = bf16[1152,512]{1,0:T(8,128)(2,1)S(1)} collective-permute-done((bf16[1152,512]{1,0:T(8,128)(2,1)S(1)}, bf16[1152,512]{1,0:T(8,128)(2,1)S(1)}, u32[]{:S(2)}, u32[]{:S(2)}) %collective-permute-start.25) | collective-permute-done | bytes 1179680 | tf_op jit(solution)/shard_map/ppermute | solution.py:84
  301.4 3.8 collective-permute-start.24
  305.3 3.8 collective-permute-start.22
  309.1 36.9 %group_product.5.rest_0_ = bf16[8192,2048]{1,0:T(8,128)(2,1)} custom-call(bf16[8192,512]{1,0:T(8,128)(2,1)} %own_m.9, bf16[1536,512]{1,0:T(8,128)(2,1)S(1)} %collective-permute-done.27.left_p, bf16[1536,512]{1,0:T(8,128)(2,1)} %collective-permute-done.28.opp_p, bf16[1536,512]{1,0:T(8,128)(2,1)} %collective-permute-done.29.right_p, bf16[8192,512]{1,0:T(8,128)(2,1)} %own_m.9, ...), custom_call_target="tpu_custom_call" | custom-call | flops 25769803776 | bytes 25165824 | tf_op jit(solution)/shard_map/group_product/pallas_call | solution.py:52
  346.0 28.5 %collective-permute-done.19.right_m = bf16[768,512]{1,0:T(8,128)(2,1)S(1)} collective-permute-done((bf16[768,512]{1,0:T(8,128)(2,1)}, bf16[768,512]{1,0:T(8,128)(2,1)S(1)}, u32[]{:S(2)}, u32[]{:S(2)}) %collective-permute-start.19) | collective-permute-done | bytes 786464 | tf_op jit(solution)/shard_map/ppermute | solution.py:84
  374.5 3.8 collective-permute-start.18
  378.4 20.8 %collective-permute-done.22.opp_p = bf16[1152,512]{1,0:T(8,128)(2,1)S(1)} collective-permute-done((bf16[1152,512]{1,0:T(8,128)(2,1)S(1)}, bf16[1152,512]{1,0:T(8,128)(2,1)S(1)}, u32[]{:S(2)}, u32[]{:S(2)}) %collective-permute-start.22) | collective-permute-done | bytes 1179680 | tf_op jit(solution)/shard_map/ppermute | solution.py:94
  399.2 0.6 collective-permute-start.16
  399.8 25.3 %collective-permute-done.26.opp_m = bf16[1152,512]{1,0:T(8,128)(2,1)S(1)} collective-permute-done((bf16[1152,512]{1,0:T(8,128)(2,1)S(1)}, bf16[1152,512]{1,0:T(8,128)(2,1)S(1)}, u32[]{:S(2)}, u32[]{:S(2)}) %collective-permute-start.26) | collective-permute-done | bytes 1179680 | tf_op jit(solution)/shard_map/ppermute | solution.py:95
  425.1 28.2 %group_product.6.rest_0_ = bf16[8192,2048]{1,0:T(8,128)(2,1)} custom-call(bf16[8192,512]{1,0:T(8,128)(2,1)} %own_m.9, bf16[1152,512]{1,0:T(8,128)(2,1)S(1)} %collective-permute-done.21.left_p, bf16[1152,512]{1,0:T(8,128)(2,1)S(1)} %collective-permute-done.22.opp_p, ...), custom_call_target="tpu_custom_call", output_to_operand_aliasing={{}: (9, {})} | custom-call | flops 19327352832 | bytes 18874368 | tf_op jit(solution)/shard_map/group_product/pallas_call | solution.py:52
  453.3 14.0 %collective-permute-done.13.right_m = bf16[384,512]{1,0:T(8,128)(2,1)S(1)} collective-permute-done((bf16[384,512]{1,0:T(8,128)(2,1)S(1)}, bf16[384,512]{1,0:T(8,128)(2,1)S(1)}, u32[]{:S(2)}, u32[]{:S(2)}) %collective-permute-start.13) | collective-permute-done | bytes 393248 | tf_op jit(solution)/shard_map/ppermute | solution.py:84
  467.3 3.8 collective-permute-start.12
  471.1 12.2 %collective-permute-done.16.opp_p = bf16[768,512]{1,0:T(8,128)(2,1)S(1)} collective-permute-done((bf16[768,512]{1,0:T(8,128)(2,1)S(1)}, bf16[768,512]{1,0:T(8,128)(2,1)S(1)}, u32[]{:S(2)}, u32[]{:S(2)}) %collective-permute-start.16) | collective-permute-done | bytes 786464 | tf_op jit(solution)/shard_map/ppermute | solution.py:94
  483.3 0.8 collective-permute-start.10
  484.1 16.9 %collective-permute-done.20.opp_m = bf16[768,512]{1,0:T(8,128)(2,1)S(1)} collective-permute-done((bf16[768,512]{1,0:T(8,128)(2,1)S(1)}, bf16[768,512]{1,0:T(8,128)(2,1)S(1)}, u32[]{:S(2)}, u32[]{:S(2)}) %collective-permute-start.20) | collective-permute-done | bytes 786464 | tf_op jit(solution)/shard_map/ppermute | solution.py:95
  501.1 19.8 %group_product.7.rest_0_ = bf16[8192,2048]{1,0:T(8,128)(2,1)} custom-call(bf16[8192,512]{1,0:T(8,128)(2,1)S(1)} %bitcast.1, bf16[768,512]{1,0:T(8,128)(2,1)S(1)} %collective-permute-done.15.left_p, bf16[768,512]{1,0:T(8,128)(2,1)S(1)} %collective-permute-done.16.opp_p, ...), custom_call_target="tpu_custom_call", output_to_operand_aliasing={{}: (9, {})} | custom-call | flops 12884901888 | bytes 12582912 | tf_op jit(solution)/shard_map/group_product/pallas_call | solution.py:52
  520.9 2.6 collective-permute-done.4.right_m
  523.5 3.8 collective-permute-start.3
  527.4 3.6 collective-permute-done.10.opp_p
  531.0 9.4 %collective-permute-done.14.opp_m = bf16[384,512]{1,0:T(8,128)(2,1)S(1)} collective-permute-done((bf16[384,512]{1,0:T(8,128)(2,1)S(1)}, bf16[384,512]{1,0:T(8,128)(2,1)S(1)}, u32[]{:S(2)}, u32[]{:S(2)}) %collective-permute-start.14) | collective-permute-done | bytes 393248 | tf_op jit(solution)/shard_map/ppermute | solution.py:95
  540.5 12.0 %group_product.8.rest_0_ = bf16[8192,2048]{1,0:T(8,128)(2,1)} custom-call(bf16[8192,512]{1,0:T(8,128)(2,1)S(1)} %bitcast.1, bf16[384,512]{1,0:T(8,128)(2,1)S(1)} %collective-permute-done.9.left_p, bf16[384,512]{1,0:T(8,128)(2,1)S(1)} %collective-permute-done.10.opp_p, ...), custom_call_target="tpu_custom_call", output_to_operand_aliasing={{}: (9, {})} | custom-call | flops 6442450944 | bytes 6291456 | tf_op jit(solution)/shard_map/group_product/pallas_call | solution.py:52
  552.4 0.7 collective-permute-done.1.opp_p
  553.2 7.9 %collective-permute-done.5.opp_m = bf16[256,512]{1,0:T(8,128)(2,1)S(1)} collective-permute-done((bf16[256,512]{1,0:T(8,128)(2,1)S(1)}, bf16[256,512]{1,0:T(8,128)(2,1)S(1)}, u32[]{:S(2)}, u32[]{:S(2)}) %collective-permute-start.5) | collective-permute-done | bytes 262176 | tf_op jit(solution)/shard_map/ppermute | solution.py:95
  561.1 9.4 %group_product.9 = bf16[8192,2048]{1,0:T(8,128)(2,1)} custom-call(bf16[8192,512]{1,0:T(8,128)(2,1)S(1)} %bitcast.1, bf16[256,512]{1,0:T(8,128)(2,1)S(1)} %collective-permute-done.left_p, bf16[256,512]{1,0:T(8,128)(2,1)S(1)} %collective-permute-done.1.opp_p, bf16[256,512]{1,0:T(8,128)(2,1)S(1)} %collective-permute-done.2.right_p, ...), custom_call_target="tpu_custom_call", output_to_operand_aliasing={{}: (9, {})} | custom-call | flops 4294967296 | bytes 4194304 | tf_op jit(solution)/shard_map/group_product/pallas_call | solution.py:52
  (60 shorter events, 1.2 us)
Async XLA Ops:
  0.0 52.4 %collective-permute-start.6 = (bf16[512,2048]{1,0:T(8,128)(2,1)}, bf16[512,2048]{1,0:T(8,128)(2,1)}, u32[]{:S(2)}, u32[]{:S(2)}) collective-permute-start(bf16[512,2048]{1,0:T(8,128)(2,1)} %param.3), channel_id=1, source_target_pairs={{0,3},{1,0},{2,1},{3,2},{4,7},{5,4},{6,5},{7,6},{8,11},{9,8},{10,9... | collective-permute-start | bytes 6291464 | tf_op jit(solution)/shard_map/ppermute | solution.py:87
  0.0 93.1 %collective-permute-start.7 = (bf16[512,2048]{1,0:T(8,128)(2,1)}, bf16[512,2048]{1,0:T(8,128)(2,1)}, u32[]{:S(2)}, u32[]{:S(2)}) collective-permute-start(bf16[512,2048]{1,0:T(8,128)(2,1)} %param.3), channel_id=1, source_target_pairs={{0,2},{1,3},{2,0},{3,1},{4,6},{5,7},{6,4},{7,5},{8,10},{9,11},{10,... | collective-permute-start | bytes 6291464 | tf_op jit(solution)/shard_map/ppermute | solution.py:87
  1.5 95.0 %collective-permute-start.8 = (bf16[512,2048]{1,0:T(8,128)(2,1)}, bf16[512,2048]{1,0:T(8,128)(2,1)}, u32[]{:S(2)}, u32[]{:S(2)}) collective-permute-start(bf16[512,2048]{1,0:T(8,128)(2,1)} %param.3), channel_id=1, source_target_pairs={{0,1},{1,2},{2,3},{3,0},{4,5},{5,6},{6,7},{7,4},{8,9},{9,10},{10,1... | collective-permute-start | bytes 6291464 | tf_op jit(solution)/shard_map/ppermute | solution.py:87
  5.2 135.3 %collective-permute-start.27 = (bf16[1536,512]{1,0:T(8,128)(2,1)}, bf16[1536,512]{1,0:T(8,128)(2,1)S(1)}, u32[]{:S(2)}, u32[]{:S(2)}) collective-permute-start(bf16[1536,512]{1,0:T(8,128)(2,1)} %get-tuple-element.6), channel_id=1, source_target_pairs={{0,4},{4,8},{8,12},{12,0},{1,5},{5,9},{9,13},{13,1},{2,6},{6,10},{... | collective-permute-start | bytes 4718600 | tf_op jit(solution)/shard_map/ppermute | solution.py:83
  7.2 89.3 %copy-start.7 = (bf16[256,512]{1,0:T(8,128)(2,1)}, bf16[256,512]{1,0:T(8,128)(2,1)S(1)}, u32[]{:S(2)}) copy-start(bf16[256,512]{1,0:T(8,128)(2,1)S(1)} %get-tuple-element.14) | copy-start | bytes 786436
  7.2 40.8 %collective-permute-start = (bf16[256,512]{1,0:T(8,128)(2,1)S(1)}, bf16[256,512]{1,0:T(8,128)(2,1)S(1)}, u32[]{:S(2)}, u32[]{:S(2)}) collective-permute-start(bf16[256,512]{1,0:T(8,128)(2,1)S(1)} %get-tuple-element.14), channel_id=1, source_target_pairs={{0,4},{4,8},{8,12},{12,0},{1,5},{5,9},{9,13},{13,1},{2,6},{6,10},{... | collective-permute-start | bytes 786440 | tf_op jit(solution)/shard_map/ppermute | solution.py:83
  48.0 92.6 %collective-permute-start.31 = (bf16[1536,512]{1,0:T(8,128)(2,1)}, bf16[1536,512]{1,0:T(8,128)(2,1)}, u32[]{:S(2)}, u32[]{:S(2)}) collective-permute-start(bf16[1536,512]{1,0:T(8,128)(2,1)} %get-tuple-element.5), channel_id=1, source_target_pairs={{0,12},{4,0},{8,4},{12,8},{1,13},{5,1},{9,5},{13,9},{2,14},{6,2},{... | collective-permute-start | bytes 4718600 | tf_op jit(solution)/shard_map/ppermute | solution.py:84
  50.4 54.0 %copy-start.4 = (bf16[384,512]{1,0:T(8,128)(2,1)}, bf16[384,512]{1,0:T(8,128)(2,1)S(1)}, u32[]{:S(2)}) copy-start(bf16[384,512]{1,0:T(8,128)(2,1)S(1)} %get-tuple-element.12) | copy-start | bytes 1179652
  50.4 92.2 %copy-start = (bf16[512,2048]{1,0:T(8,128)(2,1)S(1)}, bf16[512,2048]{1,0:T(8,128)(2,1)}, u32[]{:S(2)}) copy-start(bf16[512,2048]{1,0:T(8,128)(2,1)} %param.3) | copy-start | bytes 6291460
  52.3 91.6 %copy-start.1 = (bf16[1152,512]{1,0:T(8,128)(2,1)}, bf16[1152,512]{1,0:T(8,128)(2,1)S(1)}, u32[]{:S(2)}) copy-start(bf16[1152,512]{1,0:T(8,128)(2,1)S(1)} %get-tuple-element.8) | copy-start | bytes 3538948
  52.4 94.8 %collective-permute-start.21 = (bf16[1152,512]{1,0:T(8,128)(2,1)S(1)}, bf16[1152,512]{1,0:T(8,128)(2,1)S(1)}, u32[]{:S(2)}, u32[]{:S(2)}) collective-permute-start(bf16[1152,512]{1,0:T(8,128)(2,1)S(1)} %get-tuple-element.8), channel_id=1, source_target_pairs={{0,4},{4,8},{8,12},{12,0},{1,5},{5,9},{9,13},{13,1},{2,6},{6,10},{... | collective-permute-start | bytes 3538952 | tf_op jit(solution)/shard_map/ppermute | solution.py:83
  93.1 44.1 %collective-permute-start.15 = (bf16[768,512]{1,0:T(8,128)(2,1)}, bf16[768,512]{1,0:T(8,128)(2,1)S(1)}, u32[]{:S(2)}, u32[]{:S(2)}) collective-permute-start(bf16[768,512]{1,0:T(8,128)(2,1)} %get-tuple-element.10), channel_id=1, source_target_pairs={{0,4},{4,8},{8,12},{12,0},{1,5},{5,9},{9,13},{13,1},{2,6},{6,10},{... | collective-permute-start | bytes 2359304 | tf_op jit(solution)/shard_map/ppermute | solution.py:83
  96.5 40.2 %collective-permute-start.9 = (bf16[384,512]{1,0:T(8,128)(2,1)S(1)}, bf16[384,512]{1,0:T(8,128)(2,1)S(1)}, u32[]{:S(2)}, u32[]{:S(2)}) collective-permute-start(bf16[384,512]{1,0:T(8,128)(2,1)S(1)} %get-tuple-element.12), channel_id=1, source_target_pairs={{0,4},{4,8},{8,12},{12,0},{1,5},{5,9},{9,13},{13,1},{2,6},{6,10},{... | collective-permute-start | bytes 1179656 | tf_op jit(solution)/shard_map/ppermute | solution.py:83
  136.7 164.8 %collective-permute-start.29 = (bf16[1536,512]{1,0:T(8,128)(2,1)}, bf16[1536,512]{1,0:T(8,128)(2,1)}, u32[]{:S(2)}, u32[]{:S(2)}) collective-permute-start(bf16[1536,512]{1,0:T(8,128)(2,1)} %get-tuple-element.6), channel_id=1, source_target_pairs={{0,12},{4,0},{8,4},{12,8},{1,13},{5,1},{9,5},{13,9},{2,14},{6,2},{... | collective-permute-start | bytes 4718600 | tf_op jit(solution)/shard_map/ppermute | solution.py:97
  137.2 168.0 %collective-permute-start.30 = (bf16[1536,512]{1,0:T(8,128)(2,1)}, bf16[1536,512]{1,0:T(8,128)(2,1)}, u32[]{:S(2)}, u32[]{:S(2)}) collective-permute-start(bf16[1536,512]{1,0:T(8,128)(2,1)} %get-tuple-element.5), channel_id=1, source_target_pairs={{0,4},{4,8},{8,12},{12,0},{1,5},{5,9},{9,13},{13,1},{2,6},{6,10},{... | collective-permute-start | bytes 4718600 | tf_op jit(solution)/shard_map/ppermute | solution.py:96
  140.5 164.8 %collective-permute-start.28 = (bf16[1536,512]{1,0:T(8,128)(2,1)S(1)}, bf16[1536,512]{1,0:T(8,128)(2,1)}, u32[]{:S(2)}, u32[]{:S(2)}) collective-permute-start(bf16[1536,512]{1,0:T(8,128)(2,1)S(1)} %collective-permute-done.27.left_p), channel_id=1, source_target_pairs={{0,4},{4,8},{8,12},{12,0},{1,5},{5,9},{9,13},{13,1},{2,6},{6,10},{... | collective-permute-start | bytes 4718600 | tf_op jit(solution)/shard_map/ppermute | solution.py:94
  140.6 168.5 %collective-permute-start.32 = (bf16[1536,512]{1,0:T(8,128)(2,1)}, bf16[1536,512]{1,0:T(8,128)(2,1)}, u32[]{:S(2)}, u32[]{:S(2)}) collective-permute-start(bf16[1536,512]{1,0:T(8,128)(2,1)} %collective-permute-done.31.right_m), channel_id=1, source_target_pairs={{0,12},{4,0},{8,4},{12,8},{1,13},{5,1},{9,5},{13,9},{2,14},{6,2},{... | collective-permute-start | bytes 4718600 | tf_op jit(solution)/shard_map/ppermute | solution.py:95
  147.1 154.3 %collective-permute-start.25 = (bf16[1152,512]{1,0:T(8,128)(2,1)S(1)}, bf16[1152,512]{1,0:T(8,128)(2,1)S(1)}, u32[]{:S(2)}, u32[]{:S(2)}) collective-permute-start(bf16[1152,512]{1,0:T(8,128)(2,1)S(1)} %get-tuple-element.7), channel_id=1, source_target_pairs={{0,12},{4,0},{8,4},{12,8},{1,13},{5,1},{9,5},{13,9},{2,14},{6,2},{... | collective-permute-start | bytes 3538952 | tf_op jit(solution)/shard_map/ppermute | solution.py:84
  301.4 73.0 %collective-permute-start.23 = (bf16[1152,512]{1,0:T(8,128)(2,1)}, bf16[1152,512]{1,0:T(8,128)(2,1)S(1)}, u32[]{:S(2)}, u32[]{:S(2)}) collective-permute-start(bf16[1152,512]{1,0:T(8,128)(2,1)} %copy-done.1), channel_id=1, source_target_pairs={{0,12},{4,0},{8,4},{12,8},{1,13},{5,1},{9,5},{13,9},{2,14},{6,2},{... | collective-permute-start | bytes 3538952 | tf_op jit(solution)/shard_map/ppermute | solution.py:97
  301.4 76.9 %collective-permute-start.24 = (bf16[1152,512]{1,0:T(8,128)(2,1)S(1)}, bf16[1152,512]{1,0:T(8,128)(2,1)S(1)}, u32[]{:S(2)}, u32[]{:S(2)}) collective-permute-start(bf16[1152,512]{1,0:T(8,128)(2,1)S(1)} %get-tuple-element.7), channel_id=1, source_target_pairs={{0,4},{4,8},{8,12},{12,0},{1,5},{5,9},{9,13},{13,1},{2,6},{6,10},{... | collective-permute-start | bytes 3538952 | tf_op jit(solution)/shard_map/ppermute | solution.py:96
  305.3 69.2 %copy-start.2 = (bf16[768,512]{1,0:T(8,128)(2,1)S(1)}, bf16[768,512]{1,0:T(8,128)(2,1)}, u32[]{:S(2)}) copy-start(bf16[768,512]{1,0:T(8,128)(2,1)} %get-tuple-element.9) | copy-start | bytes 2359300
  305.3 73.0 %copy-start.3 = (bf16[384,512]{1,0:T(8,128)(2,1)S(1)}, bf16[384,512]{1,0:T(8,128)(2,1)}, u32[]{:S(2)}) copy-start(bf16[384,512]{1,0:T(8,128)(2,1)} %get-tuple-element.11) | copy-start | bytes 1179652
  305.3 69.2 %collective-permute-start.19 = (bf16[768,512]{1,0:T(8,128)(2,1)}, bf16[768,512]{1,0:T(8,128)(2,1)S(1)}, u32[]{:S(2)}, u32[]{:S(2)}) collective-permute-start(bf16[768,512]{1,0:T(8,128)(2,1)} %get-tuple-element.9), channel_id=1, source_target_pairs={{0,12},{4,0},{8,4},{12,8},{1,13},{5,1},{9,5},{13,9},{2,14},{6,2},{... | collective-permute-start | bytes 2359304 | tf_op jit(solution)/shard_map/ppermute | solution.py:84
  305.3 93.9 %collective-permute-start.22 = (bf16[1152,512]{1,0:T(8,128)(2,1)S(1)}, bf16[1152,512]{1,0:T(8,128)(2,1)S(1)}, u32[]{:S(2)}, u32[]{:S(2)}) collective-permute-start(bf16[1152,512]{1,0:T(8,128)(2,1)S(1)} %collective-permute-done.21.left_p), channel_id=1, source_target_pairs={{0,4},{4,8},{8,12},{12,0},{1,5},{5,9},{9,13},{13,1},{2,6},{6,10},{... | collective-permute-start | bytes 3538952 | tf_op jit(solution)/shard_map/ppermute | solution.py:94
  309.1 116.0 %collective-permute-start.26 = (bf16[1152,512]{1,0:T(8,128)(2,1)S(1)}, bf16[1152,512]{1,0:T(8,128)(2,1)S(1)}, u32[]{:S(2)}, u32[]{:S(2)}) collective-permute-start(bf16[1152,512]{1,0:T(8,128)(2,1)S(1)} %collective-permute-done.25.right_m), channel_id=1, source_target_pairs={{0,12},{4,0},{8,4},{12,8},{1,13},{5,1},{9,5},{13,9},{2,14},{6,2},{... | collective-permute-start | bytes 3538952 | tf_op jit(solution)/shard_map/ppermute | solution.py:95
  374.5 92.8 %collective-permute-start.17 = (bf16[768,512]{1,0:T(8,128)(2,1)}, bf16[768,512]{1,0:T(8,128)(2,1)S(1)}, u32[]{:S(2)}, u32[]{:S(2)}) collective-permute-start(bf16[768,512]{1,0:T(8,128)(2,1)} %get-tuple-element.10), channel_id=1, source_target_pairs={{0,12},{4,0},{8,4},{12,8},{1,13},{5,1},{9,5},{13,9},{2,14},{6,2},{... | collective-permute-start | bytes 2359304 | tf_op jit(solution)/shard_map/ppermute | solution.py:97
  374.5 96.6 %collective-permute-start.18 = (bf16[768,512]{1,0:T(8,128)(2,1)S(1)}, bf16[768,512]{1,0:T(8,128)(2,1)S(1)}, u32[]{:S(2)}, u32[]{:S(2)}) collective-permute-start(bf16[768,512]{1,0:T(8,128)(2,1)S(1)} %copy-done.2), channel_id=1, source_target_pairs={{0,4},{4,8},{8,12},{12,0},{1,5},{5,9},{9,13},{13,1},{2,6},{6,10},{... | collective-permute-start | bytes 2359304 | tf_op jit(solution)/shard_map/ppermute | solution.py:96
  378.3 122.8 %slice-start = ((s8[8388608]{0:T(1024)(128)(4,1)}), s8[4194304]{0:T(1024)(128)(4,1)S(1)}, s32[]{:S(2)}) async-start(s8[8388608]{0:T(1024)(128)(4,1)} %bitcast), calls=%async_computation | async-start | bytes 8388608
  378.3 88.9 %copy-start.5 = (bf16[384,512]{1,0:T(8,128)(2,1)S(1)}, bf16[384,512]{1,0:T(8,128)(2,1)}, u32[]{:S(2)}) copy-start(bf16[384,512]{1,0:T(8,128)(2,1)} %copy-done.4) | copy-start | bytes 1179652
  378.3 92.8 %copy-start.6 = (bf16[256,512]{1,0:T(8,128)(2,1)S(1)}, bf16[256,512]{1,0:T(8,128)(2,1)}, u32[]{:S(2)}) copy-start(bf16[256,512]{1,0:T(8,128)(2,1)} %get-tuple-element.13) | copy-start | bytes 786436
  378.3 122.7 %slice-start.1 = ((s8[8388608]{0:T(1024)(128)(4,1)}), s8[4194304]{0:T(1024)(128)(4,1)S(1)}, s32[]{:S(2)}) async-start(s8[8388608]{0:T(1024)(128)(4,1)} %bitcast), calls=%async_computation.1 | async-start | bytes 8388608
  378.3 88.9 %collective-permute-start.13 = (bf16[384,512]{1,0:T(8,128)(2,1)S(1)}, bf16[384,512]{1,0:T(8,128)(2,1)S(1)}, u32[]{:S(2)}, u32[]{:S(2)}) collective-permute-start(bf16[384,512]{1,0:T(8,128)(2,1)S(1)} %copy-done.3), channel_id=1, source_target_pairs={{0,12},{4,0},{8,4},{12,8},{1,13},{5,1},{9,5},{13,9},{2,14},{6,2},{... | collective-permute-start | bytes 1179656 | tf_op jit(solution)/shard_map/ppermute | solution.py:84
  399.2 84.2 %collective-permute-start.16 = (bf16[768,512]{1,0:T(8,128)(2,1)S(1)}, bf16[768,512]{1,0:T(8,128)(2,1)S(1)}, u32[]{:S(2)}, u32[]{:S(2)}) collective-permute-start(bf16[768,512]{1,0:T(8,128)(2,1)S(1)} %collective-permute-done.15.left_p), channel_id=1, source_target_pairs={{0,4},{4,8},{8,12},{12,0},{1,5},{5,9},{9,13},{13,1},{2,6},{6,10},{... | collective-permute-start | bytes 2359304 | tf_op jit(solution)/shard_map/ppermute | solution.py:94
  425.1 75.9 %collective-permute-start.20 = (bf16[768,512]{1,0:T(8,128)(2,1)S(1)}, bf16[768,512]{1,0:T(8,128)(2,1)S(1)}, u32[]{:S(2)}, u32[]{:S(2)}) collective-permute-start(bf16[768,512]{1,0:T(8,128)(2,1)S(1)} %collective-permute-done.19.right_m), channel_id=1, source_target_pairs={{0,12},{4,0},{8,4},{12,8},{1,13},{5,1},{9,5},{13,9},{2,14},{6,2},{... | collective-permute-start | bytes 2359304 | tf_op jit(solution)/shard_map/ppermute | solution.py:95
  467.2 56.3 %collective-permute-start.11 = (bf16[384,512]{1,0:T(8,128)(2,1)S(1)}, bf16[384,512]{1,0:T(8,128)(2,1)S(1)}, u32[]{:S(2)}, u32[]{:S(2)}) collective-permute-start(bf16[384,512]{1,0:T(8,128)(2,1)S(1)} %copy-done.5), channel_id=1, source_target_pairs={{0,12},{4,0},{8,4},{12,8},{1,13},{5,1},{9,5},{13,9},{2,14},{6,2},{... | collective-permute-start | bytes 1179656 | tf_op jit(solution)/shard_map/ppermute | solution.py:97
  467.3 60.1 %collective-permute-start.12 = (bf16[384,512]{1,0:T(8,128)(2,1)S(1)}, bf16[384,512]{1,0:T(8,128)(2,1)S(1)}, u32[]{:S(2)}, u32[]{:S(2)}) collective-permute-start(bf16[384,512]{1,0:T(8,128)(2,1)S(1)} %copy-done.3), channel_id=1, source_target_pairs={{0,4},{4,8},{8,12},{12,0},{1,5},{5,9},{9,13},{13,1},{2,6},{6,10},{... | collective-permute-start | bytes 1179656 | tf_op jit(solution)/shard_map/ppermute | solution.py:96
  471.1 52.4 %copy-start.8 = (bf16[256,512]{1,0:T(8,128)(2,1)S(1)}, bf16[256,512]{1,0:T(8,128)(2,1)}, u32[]{:S(2)}) copy-start(bf16[256,512]{1,0:T(8,128)(2,1)} %copy-done.7) | copy-start | bytes 786436
  471.1 52.4 %collective-permute-start.4 = (bf16[256,512]{1,0:T(8,128)(2,1)S(1)}, bf16[256,512]{1,0:T(8,128)(2,1)S(1)}, u32[]{:S(2)}, u32[]{:S(2)}) collective-permute-start(bf16[256,512]{1,0:T(8,128)(2,1)S(1)} %copy-done.6), channel_id=1, source_target_pairs={{0,12},{4,0},{8,4},{12,8},{1,13},{5,1},{9,5},{13,9},{2,14},{6,2},{... | collective-permute-start | bytes 786440 | tf_op jit(solution)/shard_map/ppermute | solution.py:84
  483.3 47.7 %collective-permute-start.10 = (bf16[384,512]{1,0:T(8,128)(2,1)S(1)}, bf16[384,512]{1,0:T(8,128)(2,1)S(1)}, u32[]{:S(2)}, u32[]{:S(2)}) collective-permute-start(bf16[384,512]{1,0:T(8,128)(2,1)S(1)} %collective-permute-done.9.left_p), channel_id=1, source_target_pairs={{0,4},{4,8},{8,12},{12,0},{1,5},{5,9},{9,13},{13,1},{2,6},{6,10},{... | collective-permute-start | bytes 1179656 | tf_op jit(solution)/shard_map/ppermute | solution.py:94
  501.0 39.4 %collective-permute-start.14 = (bf16[384,512]{1,0:T(8,128)(2,1)S(1)}, bf16[384,512]{1,0:T(8,128)(2,1)S(1)}, u32[]{:S(2)}, u32[]{:S(2)}) collective-permute-start(bf16[384,512]{1,0:T(8,128)(2,1)S(1)} %collective-permute-done.13.right_m), channel_id=1, source_target_pairs={{0,12},{4,0},{8,4},{12,8},{1,13},{5,1},{9,5},{13,9},{2,14},{6,2},{... | collective-permute-start | bytes 1179656 | tf_op jit(solution)/shard_map/ppermute | solution.py:95
  523.5 28.9 %collective-permute-start.2 = (bf16[256,512]{1,0:T(8,128)(2,1)S(1)}, bf16[256,512]{1,0:T(8,128)(2,1)S(1)}, u32[]{:S(2)}, u32[]{:S(2)}) collective-permute-start(bf16[256,512]{1,0:T(8,128)(2,1)S(1)} %copy-done.8), channel_id=1, source_target_pairs={{0,12},{4,0},{8,4},{12,8},{1,13},{5,1},{9,5},{13,9},{2,14},{6,2},{... | collective-permute-start | bytes 786440 | tf_op jit(solution)/shard_map/ppermute | solution.py:97
  523.5 28.9 %collective-permute-start.3 = (bf16[256,512]{1,0:T(8,128)(2,1)S(1)}, bf16[256,512]{1,0:T(8,128)(2,1)S(1)}, u32[]{:S(2)}, u32[]{:S(2)}) collective-permute-start(bf16[256,512]{1,0:T(8,128)(2,1)S(1)} %copy-done.6), channel_id=1, source_target_pairs={{0,4},{4,8},{8,12},{12,0},{1,5},{5,9},{9,13},{13,1},{2,6},{6,10},{... | collective-permute-start | bytes 786440 | tf_op jit(solution)/shard_map/ppermute | solution.py:96
  527.3 25.8 %collective-permute-start.1 = (bf16[256,512]{1,0:T(8,128)(2,1)S(1)}, bf16[256,512]{1,0:T(8,128)(2,1)S(1)}, u32[]{:S(2)}, u32[]{:S(2)}) collective-permute-start(bf16[256,512]{1,0:T(8,128)(2,1)S(1)} %collective-permute-done.left_p), channel_id=1, source_target_pairs={{0,4},{4,8},{8,12},{12,0},{1,5},{5,9},{9,13},{13,1},{2,6},{6,10},{... | collective-permute-start | bytes 786440 | tf_op jit(solution)/shard_map/ppermute | solution.py:94
  531.0 30.1 %collective-permute-start.5 = (bf16[256,512]{1,0:T(8,128)(2,1)S(1)}, bf16[256,512]{1,0:T(8,128)(2,1)S(1)}, u32[]{:S(2)}, u32[]{:S(2)}) collective-permute-start(bf16[256,512]{1,0:T(8,128)(2,1)S(1)} %collective-permute-done.4.right_m), channel_id=1, source_target_pairs={{0,12},{4,0},{8,4},{12,8},{1,13},{5,1},{9,5},{13,9},{2,14},{6,2},{... | collective-permute-start | bytes 786440 | tf_op jit(solution)/shard_map/ppermute | solution.py:95

commit v2 on v1

--- a/solution.py
+++ b/solution.py
@@ -8,8 +8,8 @@
 from jax.sharding import PartitionSpec as P
 
 
-GROUPS = (1536, 1152, 768, 384, 256)
-BM = 128
+GROUPS = (1536, 1024, 768, 512, 256)
+BM = 256
 
 
 def _mm_kernel(steps, own_p, left_p, opp_p, right_p, own_m, left_m, opp_m, right_m, b_ref, *rest):
@@ -68,8 +68,17 @@
 
 def solution(mesh):
     side = mesh.shape["row"]
-    up = [(p, (p + 1) % side) for p in range(side)]
-    down = [(p, (p - 1) % side) for p in range(side)]
+
+    def ring(sense):
+        pairs = []
+        for col in range(side):
+            for row in range(side):
+                step = sense if row % 2 == 0 else -sense
+                pairs.append((col * side + row, ((col + step) % side) * side + row))
+        return pairs
+
+    fwd, bwd = ring(1), ring(-1)
+    axes = ("col", "row")
 
     def local(a, b_own):
         rows, depth = a.shape
@@ -77,24 +86,25 @@
         half = rows // 2
         offs = [sum(GROUPS[:g]) for g in range(len(GROUPS))]
         row_pos, col_pos = lax.axis_index("row"), lax.axis_index("col")
+        sense = 1 - 2 * lax.rem(row_pos, 2)
 
         a_p = [lax.slice_in_dim(a, o, o + s) for o, s in zip(offs, GROUPS)]
         a_m = [lax.slice_in_dim(a, half + o, half + o + s) for o, s in zip(offs, GROUPS)]
-        left_p = [lax.ppermute(x, "col", up) for x in a_p]
-        right_m = [lax.ppermute(x, "col", down) for x in a_m]
+        left_p = [lax.ppermute(x, axes, fwd) for x in a_p]
+        right_m = [lax.ppermute(x, axes, bwd) for x in a_m]
 
-        b_all = [b_own] + [
-            lax.ppermute(b_own, "row", [(p, (p - s) % side) for p in range(side)]) for s in range(1, side)
-        ]
-        b_twice = jnp.concatenate(b_all + b_all, axis=0)
-        b = lax.dynamic_slice_in_dim(b_twice, lax.rem(col_pos - row_pos + side, side) * depth, side * depth)
+        b = jnp.zeros((side * depth, cols), b_own.dtype)
+        for s in range(side):
+            blk = b_own if s == 0 else lax.ppermute(b_own, "row", [(p, (p - s) % side) for p in range(side)])
+            place = lax.rem((row_pos + s - col_pos) * sense + 2 * side, side)
+            b = lax.dynamic_update_slice_in_dim(b, blk, place * depth, 0)
 
         c = None
         for g, (off, size) in enumerate(zip(offs, GROUPS)):
-            opp_p = lax.ppermute(left_p[g], "col", up)
-            opp_m = lax.ppermute(right_m[g], "col", down)
-            left_m = lax.ppermute(a_m[g], "col", up)
-            right_p = lax.ppermute(a_p[g], "col", down)
+            opp_p = lax.ppermute(left_p[g], axes, fwd)
+            opp_m = lax.ppermute(right_m[g], axes, bwd)
+            left_m = lax.ppermute(a_m[g], axes, fwd)
+            right_p = lax.ppermute(a_p[g], axes, bwd)
             c = _group_product(
                 a, left_p[g], opp_p, right_p, left_m, opp_m, right_m[g], b, c, rows, cols, off, size, half
             )

time: 573 us -> 563 us (0.983)
  starting transfers between devices: 35.5 us -> 109 us
  waiting for transfers between devices: 385 us -> 328 us
  local copies, waits for them, and re-layouts: 44 us -> 24.8 us
  Pallas kernels: 106 us -> 99.2 us
    ppermute x30, starting transfers between devices: 34 us -> 107 us  [the longest x5 61.5 us: local(): right_p = lax.ppermute(a_p[g], axes, bwd)]
    ppermute x3, waiting for transfers between devices: 37.3 us -> 0.01 us  [local(): lax.ppermute(b_own, 'row', [(p, (p - s) % side) for p in range(side)])]
    ppermute x30, waiting for transfers between devices: 347 us -> 328 us  [the longest x5 182 us: local(): right_m = [lax.ppermute(x, axes, bwd) for x in a_m]]
    unnamed x29 -> x24, local copies, waits for them, and re-layouts: 20.4 us -> 3.35 us
    dynamic_slice x1 -> x0, local copies, waits for them, and re-layouts: 8.35 us -> none  [local(): lax.dynamic_slice_in_dim(b_twice, lax.rem(col_pos - row_pos + side, side)...]
    dynamic_update_slice x0 -> x4, local copies, waits for them, and re-layouts: none -> 7.68 us  [local(): b = lax.dynamic_update_slice_in_dim(b, blk, place * depth, 0)]
    pallas_call x5, Pallas kernels: 106 us -> 99.2 us  [_group_product(): pl.pallas_call(functools.partial(_mm_kernel, steps), grid=(2 * steps,), o...]
  transfers between devices with their start and end apart: 33 -> 33, of which waited for: 15 -> 11; matrix products, arithmetic and copies ran while one was open for 8% -> 3% of each run, Pallas kernels for 17% -> 16%
where the time goes in v2:
time: 563 us; the launch traced here: 561 us
  waiting for transfers between devices  328 us (58%)
  starting transfers between devices  109 us (19%)
  Pallas kernels  99.2 us (18%)
  local copies, waits for them, and re-layouts  24.8 us (4%)
    ppermute x5, waiting for transfers between devices, local(): right_m = [lax.ppermute(x, axes, bwd) for x in a_m]  182 us
    ppermute x5, waiting for transfers between devices, local(): left_p = [lax.ppermute(x, axes, fwd) for x in a_p]  113 us
    pallas_call x5, Pallas kernels, _group_product(): pl.pallas_call(functools.partial(_mm_kernel, steps), grid=(2 * steps,), o...  99.2 us
    ppermute x5, starting transfers between devices, local(): right_p = lax.ppermute(a_p[g], axes, bwd)  61.5 us
    ppermute x5, waiting for transfers between devices, local(): opp_m = lax.ppermute(right_m[g], axes, bwd)  27.1 us
    ppermute x5, starting transfers between devices, local(): opp_m = lax.ppermute(right_m[g], axes, bwd)  17.3 us
    slice x5, local copies, waits for them, and re-layouts, local(): lax.slice_in_dim(a, half + o, half + o + s)  12.7 us
  transfers between devices with their start and end apart: 33, of which 11 were waited for; matrix products, arithmetic and copies ran while one was open for 3% of the time, Pallas kernels for 16%

profile of v2, /device:TPU:28, one launch (start us, length us, event | category | flops | bytes accessed | tf_op | source)
XLA Modules:
  0.0 560.5 jit_solution(5180922342088573691)
XLA Ops:
  0.0 2.7 fusion.1
  2.9 2.2 fusion.3
  5.1 1.4 collective-permute-start.9
  6.5 1.8 fusion.4
  8.3 1.6 collective-permute-start
  9.9 2.4 fusion.2
  12.2 1.6 collective-permute-start.15
  13.8 31.1 %collective-permute-done.left_p = bf16[256,512]{1,0:T(8,128)(2,1)S(1)} collective-permute-done((bf16[256,512]{1,0:T(8,128)(2,1)S(1)}, bf16[256,512]{1,0:T(8,128)(2,1)S(1)}, u32[]{:S(2)}, u32[]{:S(2)}) %collective-permute-start) | collective-permute-done | bytes 262176 | tf_op jit(solution)/shard_map/ppermute | solution.py:93
  45.4 0.9 collective-permute-start.8
  46.3 3.7 fusion
  50.1 12.3 %collective-permute-done.15.left_p = bf16[768,512]{1,0:T(8,128)(2,1)S(1)} collective-permute-done((bf16[768,512]{1,0:T(8,128)(2,1)}, bf16[768,512]{1,0:T(8,128)(2,1)S(1)}, u32[]{:S(2)}, u32[]{:S(2)}) %collective-permute-start.15) | collective-permute-done | bytes 786464 | tf_op jit(solution)/shard_map/ppermute | solution.py:93
  62.4 1.1 collective-permute-start.27
  64.5 69.3 %collective-permute-done.27.left_p = bf16[1536,512]{1,0:T(8,128)(2,1)} collective-permute-done((bf16[1536,512]{1,0:T(8,128)(2,1)}, bf16[1536,512]{1,0:T(8,128)(2,1)}, u32[]{:S(2)}, u32[]{:S(2)}) %collective-permute-start.27) | collective-permute-done | bytes 1572896 | tf_op jit(solution)/shard_map/ppermute | solution.py:93
  133.9 3.6 collective-permute-start.30
  137.6 2.0 collective-permute-start.32
  139.6 1.1 broadcast_in_dim.3
  140.7 2.0 constant_dynamic-update-slice_fusion.3
  142.7 1.9 constant_dynamic-update-slice_fusion.2
  144.6 1.9 constant_dynamic-update-slice_fusion.1
  146.5 1.9 constant_dynamic-update-slice_fusion.b_ref
  148.4 3.3 copy-done
  151.7 141.1 %collective-permute-done.25.right_m = bf16[1024,512]{1,0:T(8,128)(2,1)S(1)} collective-permute-done((bf16[1024,512]{1,0:T(8,128)(2,1)}, bf16[1024,512]{1,0:T(8,128)(2,1)S(1)}, u32[]{:S(2)}, u32[]{:S(2)}) %collective-permute-start.25) | collective-permute-done | bytes 1048608 | tf_op jit(solution)/shard_map/ppermute | solution.py:94
  292.8 11.4 %collective-permute-start.23 = (bf16[1024,512]{1,0:T(8,128)(2,1)S(1)}, bf16[1024,512]{1,0:T(8,128)(2,1)S(1)}, u32[]{:S(2)}, u32[]{:S(2)}) collective-permute-start(bf16[1024,512]{1,0:T(8,128)(2,1)S(1)} %copy-done.3), channel_id=1, source_target_pairs={{0,12},{1,5},{2,14},{3,7},{4,0},{5,9},{6,2},{7,11},{8,4},{9,13},{1... | collective-permute-start | bytes 3145736 | tf_op jit(solution)/shard_map/ppermute | solution.py:107
  304.7 1.9 collective-permute-start.19
  306.7 1.9 collective-permute-start.22
  308.7 34.1 %group_product.5.rest_0_ = bf16[8192,2048]{1,0:T(8,128)(2,1)} custom-call(bf16[8192,512]{1,0:T(8,128)(2,1)} %own_m.9, bf16[1536,512]{1,0:T(8,128)(2,1)} %collective-permute-done.27.left_p, bf16[1536,512]{1,0:T(8,128)(2,1)} %collective-permute-done.28.opp_p, bf16[1536,512]{1,0:T(8,128)(2,1)} %collective-permute-done.29.right_p, bf16[8192,512]{1,0:T(8,128)(2,1)} %own_m.9, ...), custom_call_target="tpu_custom_call" | custom-call | flops 25769803776 | bytes 25165824 | tf_op jit(solution)/shard_map/group_product/pallas_call | solution.py:52
  342.8 25.2 %collective-permute-done.19.right_m = bf16[768,512]{1,0:T(8,128)(2,1)S(1)} collective-permute-done((bf16[768,512]{1,0:T(8,128)(2,1)S(1)}, bf16[768,512]{1,0:T(8,128)(2,1)S(1)}, u32[]{:S(2)}, u32[]{:S(2)}) %collective-permute-start.19) | collective-permute-done | bytes 786464 | tf_op jit(solution)/shard_map/ppermute | solution.py:94
  368.0 29.5 %collective-permute-start.17 = (bf16[768,512]{1,0:T(8,128)(2,1)}, bf16[768,512]{1,0:T(8,128)(2,1)S(1)}, u32[]{:S(2)}, u32[]{:S(2)}) collective-permute-start(bf16[768,512]{1,0:T(8,128)(2,1)} %get-tuple-element.10), channel_id=1, source_target_pairs={{0,12},{1,5},{2,14},{3,7},{4,0},{5,9},{6,2},{7,11},{8,4},{9,13},{1... | collective-permute-start | bytes 2359304 | tf_op jit(solution)/shard_map/ppermute | solution.py:107
  397.5 1.4 collective-permute-start.18
  398.9 1.2 collective-permute-start.13
  400.1 2.7 collective-permute-start.16
  402.8 10.3 %collective-permute-done.26.opp_m = bf16[1024,512]{1,0:T(8,128)(2,1)S(1)} collective-permute-done((bf16[1024,512]{1,0:T(8,128)(2,1)S(1)}, bf16[1024,512]{1,0:T(8,128)(2,1)S(1)}, u32[]{:S(2)}, u32[]{:S(2)}) %collective-permute-start.26) | collective-permute-done | bytes 1048608 | tf_op jit(solution)/shard_map/ppermute | solution.py:105
  413.1 12.5 %collective-permute-start.20 = (bf16[768,512]{1,0:T(8,128)(2,1)S(1)}, bf16[768,512]{1,0:T(8,128)(2,1)S(1)}, u32[]{:S(2)}, u32[]{:S(2)}) collective-permute-start(bf16[768,512]{1,0:T(8,128)(2,1)S(1)} %collective-permute-done.19.right_m), channel_id=1, source_target_pairs={{0,12},{1,5},{2,14},{3,7},{4,0},{5,9},{6,2},{7,11},{8,4},{9,13},{1... | collective-permute-start | bytes 2359304 | tf_op jit(solution)/shard_map/ppermute | solution.py:105
  425.6 23.6 %group_product.6.rest_0_ = bf16[8192,2048]{1,0:T(8,128)(2,1)} custom-call(bf16[8192,512]{1,0:T(8,128)(2,1)} %own_m.9, bf16[1024,512]{1,0:T(8,128)(2,1)S(1)} %collective-permute-done.21.left_p, bf16[1024,512]{1,0:T(8,128)(2,1)S(1)} %collective-permute-done.22.opp_p, ...), custom_call_target="tpu_custom_call", output_to_operand_aliasing={{}: (9, {})} | custom-call | flops 17179869184 | bytes 16777216 | tf_op jit(solution)/shard_map/group_product/pallas_call | solution.py:52
  449.2 8.8 %collective-permute-done.13.right_m = bf16[512,512]{1,0:T(8,128)(2,1)S(1)} collective-permute-done((bf16[512,512]{1,0:T(8,128)(2,1)S(1)}, bf16[512,512]{1,0:T(8,128)(2,1)S(1)}, u32[]{:S(2)}, u32[]{:S(2)}) %collective-permute-start.13) | collective-permute-done | bytes 524320 | tf_op jit(solution)/shard_map/ppermute | solution.py:94
  458.0 18.9 %collective-permute-start.11 = (bf16[512,512]{1,0:T(8,128)(2,1)S(1)}, bf16[512,512]{1,0:T(8,128)(2,1)S(1)}, u32[]{:S(2)}, u32[]{:S(2)}) collective-permute-start(bf16[512,512]{1,0:T(8,128)(2,1)S(1)} %copy-done.6), channel_id=1, source_target_pairs={{0,12},{1,5},{2,14},{3,7},{4,0},{5,9},{6,2},{7,11},{8,4},{9,13},{1... | collective-permute-start | bytes 1572872 | tf_op jit(solution)/shard_map/ppermute | solution.py:107
  476.9 2.1 collective-permute-start.12
  479.4 3.4 collective-permute-start.10
  482.8 8.9 %collective-permute-done.20.opp_m = bf16[768,512]{1,0:T(8,128)(2,1)S(1)} collective-permute-done((bf16[768,512]{1,0:T(8,128)(2,1)S(1)}, bf16[768,512]{1,0:T(8,128)(2,1)S(1)}, u32[]{:S(2)}, u32[]{:S(2)}) %collective-permute-start.20) | collective-permute-done | bytes 786464 | tf_op jit(solution)/shard_map/ppermute | solution.py:105
  491.7 2.3 collective-permute-start.14
  494.0 18.6 %group_product.7.rest_0_ = bf16[8192,2048]{1,0:T(8,128)(2,1)} custom-call(bf16[8192,512]{1,0:T(8,128)(2,1)S(1)} %bitcast.1, bf16[768,512]{1,0:T(8,128)(2,1)S(1)} %collective-permute-done.15.left_p, bf16[768,512]{1,0:T(8,128)(2,1)S(1)} %collective-permute-done.16.opp_p, ...), custom_call_target="tpu_custom_call", output_to_operand_aliasing={{}: (9, {})} | custom-call | flops 12884901888 | bytes 12582912 | tf_op jit(solution)/shard_map/group_product/pallas_call | solution.py:52
  512.5 7.4 %collective-permute-done.4.right_m = bf16[256,512]{1,0:T(8,128)(2,1)S(1)} collective-permute-done((bf16[256,512]{1,0:T(8,128)(2,1)S(1)}, bf16[256,512]{1,0:T(8,128)(2,1)S(1)}, u32[]{:S(2)}, u32[]{:S(2)}) %collective-permute-start.4) | collective-permute-done | bytes 262176 | tf_op jit(solution)/shard_map/ppermute | solution.py:94
  519.9 1.5 collective-permute-start.2
  521.4 2.3 collective-permute-start.3
  523.8 5.5 collective-permute-done.10.opp_p
  529.7 7.9 %collective-permute-done.14.opp_m = bf16[512,512]{1,0:T(8,128)(2,1)S(1)} collective-permute-done((bf16[512,512]{1,0:T(8,128)(2,1)S(1)}, bf16[512,512]{1,0:T(8,128)(2,1)S(1)}, u32[]{:S(2)}, u32[]{:S(2)}) %collective-permute-start.14) | collective-permute-done | bytes 524320 | tf_op jit(solution)/shard_map/ppermute | solution.py:105
  537.6 13.8 %group_product.8.rest_0_ = bf16[8192,2048]{1,0:T(8,128)(2,1)} custom-call(bf16[8192,512]{1,0:T(8,128)(2,1)S(1)} %bitcast.1, bf16[512,512]{1,0:T(8,128)(2,1)S(1)} %collective-permute-done.9.left_p, bf16[512,512]{1,0:T(8,128)(2,1)S(1)} %collective-permute-done.10.opp_p, ...), custom_call_target="tpu_custom_call", output_to_operand_aliasing={{}: (9, {})} | custom-call | flops 8589934592 | bytes 8388608 | tf_op jit(solution)/shard_map/group_product/pallas_call | solution.py:52
  551.4 9.1 %group_product.9 = bf16[8192,2048]{1,0:T(8,128)(2,1)} custom-call(bf16[8192,512]{1,0:T(8,128)(2,1)S(1)} %bitcast.1, bf16[256,512]{1,0:T(8,128)(2,1)S(1)} %collective-permute-done.left_p, bf16[256,512]{1,0:T(8,128)(2,1)S(1)} %collective-permute-done.1.opp_p, bf16[256,512]{1,0:T(8,128)(2,1)S(1)} %collective-permute-done.2.right_p, ...), custom_call_target="tpu_custom_call", output_to_operand_aliasing={{}: (9, {})} | custom-call | flops 4294967296 | bytes 4194304 | tf_op jit(solution)/shard_map/group_product/pallas_call | solution.py:52
  (58 shorter events, 3.6 us)
Async XLA Ops:
  2.7 60.9 %copy-start.2 = (bf16[1024,512]{1,0:T(8,128)(2,1)}, bf16[1024,512]{1,0:T(8,128)(2,1)S(1)}, u32[]{:S(2)}) copy-start(bf16[1024,512]{1,0:T(8,128)(2,1)S(1)} %get-tuple-element.8) | copy-start | bytes 3145732
  2.7 60.9 %collective-permute-start.21 = (bf16[1024,512]{1,0:T(8,128)(2,1)S(1)}, bf16[1024,512]{1,0:T(8,128)(2,1)S(1)}, u32[]{:S(2)}, u32[]{:S(2)}) collective-permute-start(bf16[1024,512]{1,0:T(8,128)(2,1)S(1)} %get-tuple-element.8), channel_id=1, source_target_pairs={{0,4},{1,13},{2,6},{3,15},{4,8},{5,1},{6,10},{7,3},{8,12},{9,5},{1... | collective-permute-start | bytes 3145736 | tf_op jit(solution)/shard_map/ppermute | solution.py:93
  5.1 40.3 %copy-start.5 = (bf16[512,512]{1,0:T(8,128)(2,1)}, bf16[512,512]{1,0:T(8,128)(2,1)S(1)}, u32[]{:S(2)}) copy-start(bf16[512,512]{1,0:T(8,128)(2,1)S(1)} %get-tuple-element.12) | copy-start | bytes 1572868
  5.1 40.3 %collective-permute-start.9 = (bf16[512,512]{1,0:T(8,128)(2,1)S(1)}, bf16[512,512]{1,0:T(8,128)(2,1)S(1)}, u32[]{:S(2)}, u32[]{:S(2)}) collective-permute-start(bf16[512,512]{1,0:T(8,128)(2,1)S(1)} %get-tuple-element.12), channel_id=1, source_target_pairs={{0,4},{1,13},{2,6},{3,15},{4,8},{5,1},{6,10},{7,3},{8,12},{9,5},{1... | collective-permute-start | bytes 1572872 | tf_op jit(solution)/shard_map/ppermute | solution.py:93
  8.3 37.1 %copy-start.8 = (bf16[256,512]{1,0:T(8,128)(2,1)}, bf16[256,512]{1,0:T(8,128)(2,1)S(1)}, u32[]{:S(2)}) copy-start(bf16[256,512]{1,0:T(8,128)(2,1)S(1)} %get-tuple-element.14) | copy-start | bytes 786436
  8.3 36.6 %collective-permute-start = (bf16[256,512]{1,0:T(8,128)(2,1)S(1)}, bf16[256,512]{1,0:T(8,128)(2,1)S(1)}, u32[]{:S(2)}, u32[]{:S(2)}) collective-permute-start(bf16[256,512]{1,0:T(8,128)(2,1)S(1)} %get-tuple-element.14), channel_id=1, source_target_pairs={{0,4},{1,13},{2,6},{3,15},{4,8},{5,1},{6,10},{7,3},{8,12},{9,5},{1... | collective-permute-start | bytes 786440 | tf_op jit(solution)/shard_map/ppermute | solution.py:93
  12.2 50.2 %collective-permute-start.15 = (bf16[768,512]{1,0:T(8,128)(2,1)}, bf16[768,512]{1,0:T(8,128)(2,1)S(1)}, u32[]{:S(2)}, u32[]{:S(2)}) collective-permute-start(bf16[768,512]{1,0:T(8,128)(2,1)} %get-tuple-element.10), channel_id=1, source_target_pairs={{0,4},{1,13},{2,6},{3,15},{4,8},{5,1},{6,10},{7,3},{8,12},{9,5},{1... | collective-permute-start | bytes 2359304 | tf_op jit(solution)/shard_map/ppermute | solution.py:93
  13.8 123.7 %collective-permute-start.6 = (bf16[512,2048]{1,0:T(8,128)(2,1)}, bf16[512,2048]{1,0:T(8,128)(2,1)}, u32[]{:S(2)}, u32[]{:S(2)}) collective-permute-start(bf16[512,2048]{1,0:T(8,128)(2,1)} %param.3), channel_id=1, source_target_pairs={{0,3},{1,0},{2,1},{3,2},{4,7},{5,4},{6,5},{7,6},{8,11},{9,8},{10,9... | collective-permute-start | bytes 6291464 | tf_op jit(solution)/shard_map/ppermute | solution.py:98
  44.9 92.7 %collective-permute-start.7 = (bf16[512,2048]{1,0:T(8,128)(2,1)}, bf16[512,2048]{1,0:T(8,128)(2,1)}, u32[]{:S(2)}, u32[]{:S(2)}) collective-permute-start(bf16[512,2048]{1,0:T(8,128)(2,1)} %param.3), channel_id=1, source_target_pairs={{0,2},{1,3},{2,0},{3,1},{4,6},{5,7},{6,4},{7,5},{8,10},{9,11},{10,... | collective-permute-start | bytes 6291464 | tf_op jit(solution)/shard_map/ppermute | solution.py:98
  45.4 94.2 %collective-permute-start.8 = (bf16[512,2048]{1,0:T(8,128)(2,1)}, bf16[512,2048]{1,0:T(8,128)(2,1)}, u32[]{:S(2)}, u32[]{:S(2)}) collective-permute-start(bf16[512,2048]{1,0:T(8,128)(2,1)} %param.3), channel_id=1, source_target_pairs={{0,1},{1,2},{2,3},{3,0},{4,5},{5,6},{6,7},{7,4},{8,9},{9,10},{10,1... | collective-permute-start | bytes 6291464 | tf_op jit(solution)/shard_map/ppermute | solution.py:98
  62.4 71.3 %collective-permute-start.27 = (bf16[1536,512]{1,0:T(8,128)(2,1)}, bf16[1536,512]{1,0:T(8,128)(2,1)}, u32[]{:S(2)}, u32[]{:S(2)}) collective-permute-start(bf16[1536,512]{1,0:T(8,128)(2,1)} %get-tuple-element.6), channel_id=1, source_target_pairs={{0,4},{1,13},{2,6},{3,15},{4,8},{5,1},{6,10},{7,3},{8,12},{9,5},{1... | collective-permute-start | bytes 4718600 | tf_op jit(solution)/shard_map/ppermute | solution.py:93
  63.5 70.4 %collective-permute-start.31 = (bf16[1536,512]{1,0:T(8,128)(2,1)}, bf16[1536,512]{1,0:T(8,128)(2,1)}, u32[]{:S(2)}, u32[]{:S(2)}) collective-permute-start(bf16[1536,512]{1,0:T(8,128)(2,1)} %get-tuple-element.5), channel_id=1, source_target_pairs={{0,12},{1,5},{2,14},{3,7},{4,0},{5,9},{6,2},{7,11},{8,4},{9,13},{1... | collective-permute-start | bytes 4718600 | tf_op jit(solution)/shard_map/ppermute | solution.py:94
  133.7 170.5 %collective-permute-start.29 = (bf16[1536,512]{1,0:T(8,128)(2,1)}, bf16[1536,512]{1,0:T(8,128)(2,1)}, u32[]{:S(2)}, u32[]{:S(2)}) collective-permute-start(bf16[1536,512]{1,0:T(8,128)(2,1)} %get-tuple-element.6), channel_id=1, source_target_pairs={{0,12},{1,5},{2,14},{3,7},{4,0},{5,9},{6,2},{7,11},{8,4},{9,13},{1... | collective-permute-start | bytes 4718600 | tf_op jit(solution)/shard_map/ppermute | solution.py:107
  133.9 170.8 %collective-permute-start.30 = (bf16[1536,512]{1,0:T(8,128)(2,1)}, bf16[1536,512]{1,0:T(8,128)(2,1)}, u32[]{:S(2)}, u32[]{:S(2)}) collective-permute-start(bf16[1536,512]{1,0:T(8,128)(2,1)} %get-tuple-element.5), channel_id=1, source_target_pairs={{0,4},{1,13},{2,6},{3,15},{4,8},{5,1},{6,10},{7,3},{8,12},{9,5},{1... | collective-permute-start | bytes 4718600 | tf_op jit(solution)/shard_map/ppermute | solution.py:106
  137.5 169.1 %collective-permute-start.28 = (bf16[1536,512]{1,0:T(8,128)(2,1)}, bf16[1536,512]{1,0:T(8,128)(2,1)}, u32[]{:S(2)}, u32[]{:S(2)}) collective-permute-start(bf16[1536,512]{1,0:T(8,128)(2,1)} %collective-permute-done.27.left_p), channel_id=1, source_target_pairs={{0,4},{1,13},{2,6},{3,15},{4,8},{5,1},{6,10},{7,3},{8,12},{9,5},{1... | collective-permute-start | bytes 4718600 | tf_op jit(solution)/shard_map/ppermute | solution.py:104
  137.6 171.0 %collective-permute-start.32 = (bf16[1536,512]{1,0:T(8,128)(2,1)}, bf16[1536,512]{1,0:T(8,128)(2,1)}, u32[]{:S(2)}, u32[]{:S(2)}) collective-permute-start(bf16[1536,512]{1,0:T(8,128)(2,1)} %collective-permute-done.31.right_m), channel_id=1, source_target_pairs={{0,12},{1,5},{2,14},{3,7},{4,0},{5,9},{6,2},{7,11},{8,4},{9,13},{1... | collective-permute-start | bytes 4718600 | tf_op jit(solution)/shard_map/ppermute | solution.py:105
  139.6 153.2 %collective-permute-start.25 = (bf16[1024,512]{1,0:T(8,128)(2,1)}, bf16[1024,512]{1,0:T(8,128)(2,1)S(1)}, u32[]{:S(2)}, u32[]{:S(2)}) collective-permute-start(bf16[1024,512]{1,0:T(8,128)(2,1)} %get-tuple-element.7), channel_id=1, source_target_pairs={{0,12},{1,5},{2,14},{3,7},{4,0},{5,9},{6,2},{7,11},{8,4},{9,13},{1... | collective-permute-start | bytes 3145736 | tf_op jit(solution)/shard_map/ppermute | solution.py:94
  140.7 152.1 %copy-start.3 = (bf16[1024,512]{1,0:T(8,128)(2,1)S(1)}, bf16[1024,512]{1,0:T(8,128)(2,1)}, u32[]{:S(2)}) copy-start(bf16[1024,512]{1,0:T(8,128)(2,1)} %copy-done.2) | copy-start | bytes 3145732
  140.7 163.5 %copy-start.1 = (bf16[1024,512]{1,0:T(8,128)(2,1)S(1)}, bf16[1024,512]{1,0:T(8,128)(2,1)}, u32[]{:S(2)}) copy-start(bf16[1024,512]{1,0:T(8,128)(2,1)} %get-tuple-element.7) | copy-start | bytes 3145732
  148.4 3.3 copy-start
  292.8 104.7 %collective-permute-start.23 = (bf16[1024,512]{1,0:T(8,128)(2,1)S(1)}, bf16[1024,512]{1,0:T(8,128)(2,1)S(1)}, u32[]{:S(2)}, u32[]{:S(2)}) collective-permute-start(bf16[1024,512]{1,0:T(8,128)(2,1)S(1)} %copy-done.3), channel_id=1, source_target_pairs={{0,12},{1,5},{2,14},{3,7},{4,0},{5,9},{6,2},{7,11},{8,4},{9,13},{1... | collective-permute-start | bytes 3145736 | tf_op jit(solution)/shard_map/ppermute | solution.py:107
  304.2 94.7 %collective-permute-start.24 = (bf16[1024,512]{1,0:T(8,128)(2,1)S(1)}, bf16[1024,512]{1,0:T(8,128)(2,1)S(1)}, u32[]{:S(2)}, u32[]{:S(2)}) collective-permute-start(bf16[1024,512]{1,0:T(8,128)(2,1)S(1)} %copy-done.1), channel_id=1, source_target_pairs={{0,4},{1,13},{2,6},{3,15},{4,8},{5,1},{6,10},{7,3},{8,12},{9,5},{1... | collective-permute-start | bytes 3145736 | tf_op jit(solution)/shard_map/ppermute | solution.py:106
  304.7 94.2 %copy-start.4 = (bf16[512,512]{1,0:T(8,128)(2,1)S(1)}, bf16[512,512]{1,0:T(8,128)(2,1)}, u32[]{:S(2)}) copy-start(bf16[512,512]{1,0:T(8,128)(2,1)} %get-tuple-element.11) | copy-start | bytes 1572868
  304.7 63.3 %collective-permute-start.19 = (bf16[768,512]{1,0:T(8,128)(2,1)S(1)}, bf16[768,512]{1,0:T(8,128)(2,1)S(1)}, u32[]{:S(2)}, u32[]{:S(2)}) collective-permute-start(bf16[768,512]{1,0:T(8,128)(2,1)S(1)} %get-tuple-element.9), channel_id=1, source_target_pairs={{0,12},{1,5},{2,14},{3,7},{4,0},{5,9},{6,2},{7,11},{8,4},{9,13},{1... | collective-permute-start | bytes 2359304 | tf_op jit(solution)/shard_map/ppermute | solution.py:94
  306.7 93.5 %collective-permute-start.22 = (bf16[1024,512]{1,0:T(8,128)(2,1)S(1)}, bf16[1024,512]{1,0:T(8,128)(2,1)S(1)}, u32[]{:S(2)}, u32[]{:S(2)}) collective-permute-start(bf16[1024,512]{1,0:T(8,128)(2,1)S(1)} %collective-permute-done.21.left_p), channel_id=1, source_target_pairs={{0,4},{1,13},{2,6},{3,15},{4,8},{5,1},{6,10},{7,3},{8,12},{9,5},{1... | collective-permute-start | bytes 3145736 | tf_op jit(solution)/shard_map/ppermute | solution.py:104
  308.6 104.5 %collective-permute-start.26 = (bf16[1024,512]{1,0:T(8,128)(2,1)S(1)}, bf16[1024,512]{1,0:T(8,128)(2,1)S(1)}, u32[]{:S(2)}, u32[]{:S(2)}) collective-permute-start(bf16[1024,512]{1,0:T(8,128)(2,1)S(1)} %collective-permute-done.25.right_m), channel_id=1, source_target_pairs={{0,12},{1,5},{2,14},{3,7},{4,0},{5,9},{6,2},{7,11},{8,4},{9,13},{1... | collective-permute-start | bytes 3145736 | tf_op jit(solution)/shard_map/ppermute | solution.py:105
  368.0 108.8 %collective-permute-start.17 = (bf16[768,512]{1,0:T(8,128)(2,1)}, bf16[768,512]{1,0:T(8,128)(2,1)S(1)}, u32[]{:S(2)}, u32[]{:S(2)}) collective-permute-start(bf16[768,512]{1,0:T(8,128)(2,1)} %get-tuple-element.10), channel_id=1, source_target_pairs={{0,12},{1,5},{2,14},{3,7},{4,0},{5,9},{6,2},{7,11},{8,4},{9,13},{1... | collective-permute-start | bytes 2359304 | tf_op jit(solution)/shard_map/ppermute | solution.py:107
  397.5 81.4 %collective-permute-start.18 = (bf16[768,512]{1,0:T(8,128)(2,1)S(1)}, bf16[768,512]{1,0:T(8,128)(2,1)S(1)}, u32[]{:S(2)}, u32[]{:S(2)}) collective-permute-start(bf16[768,512]{1,0:T(8,128)(2,1)S(1)} %get-tuple-element.9), channel_id=1, source_target_pairs={{0,4},{1,13},{2,6},{3,15},{4,8},{5,1},{6,10},{7,3},{8,12},{9,5},{1... | collective-permute-start | bytes 2359304 | tf_op jit(solution)/shard_map/ppermute | solution.py:106
  398.9 95.1 %slice-start = ((s8[8388608]{0:T(1024)(128)(4,1)}), s8[4194304]{0:T(1024)(128)(4,1)S(1)}, s32[]{:S(2)}) async-start(s8[8388608]{0:T(1024)(128)(4,1)} %bitcast), calls=%async_computation | async-start | bytes 8388608
  398.9 59.1 %copy-start.6 = (bf16[512,512]{1,0:T(8,128)(2,1)S(1)}, bf16[512,512]{1,0:T(8,128)(2,1)}, u32[]{:S(2)}) copy-start(bf16[512,512]{1,0:T(8,128)(2,1)} %copy-done.5) | copy-start | bytes 1572868
  398.9 80.0 %copy-start.7 = (bf16[256,512]{1,0:T(8,128)(2,1)S(1)}, bf16[256,512]{1,0:T(8,128)(2,1)}, u32[]{:S(2)}) copy-start(bf16[256,512]{1,0:T(8,128)(2,1)} %get-tuple-element.13) | copy-start | bytes 786436
  398.9 95.1 %slice-start.1 = ((s8[8388608]{0:T(1024)(128)(4,1)}), s8[4194304]{0:T(1024)(128)(4,1)S(1)}, s32[]{:S(2)}) async-start(s8[8388608]{0:T(1024)(128)(4,1)} %bitcast), calls=%async_computation.1 | async-start | bytes 8388608
  398.9 59.0 %collective-permute-start.13 = (bf16[512,512]{1,0:T(8,128)(2,1)S(1)}, bf16[512,512]{1,0:T(8,128)(2,1)S(1)}, u32[]{:S(2)}, u32[]{:S(2)}) collective-permute-start(bf16[512,512]{1,0:T(8,128)(2,1)S(1)} %copy-done.4), channel_id=1, source_target_pairs={{0,12},{1,5},{2,14},{3,7},{4,0},{5,9},{6,2},{7,11},{8,4},{9,13},{1... | collective-permute-start | bytes 1572872 | tf_op jit(solution)/shard_map/ppermute | solution.py:94
  400.1 79.3 %collective-permute-start.16 = (bf16[768,512]{1,0:T(8,128)(2,1)S(1)}, bf16[768,512]{1,0:T(8,128)(2,1)S(1)}, u32[]{:S(2)}, u32[]{:S(2)}) collective-permute-start(bf16[768,512]{1,0:T(8,128)(2,1)S(1)} %collective-permute-done.15.left_p), channel_id=1, source_target_pairs={{0,4},{1,13},{2,6},{3,15},{4,8},{5,1},{6,10},{7,3},{8,12},{9,5},{1... | collective-permute-start | bytes 2359304 | tf_op jit(solution)/shard_map/ppermute | solution.py:104
  413.1 78.6 %collective-permute-start.20 = (bf16[768,512]{1,0:T(8,128)(2,1)S(1)}, bf16[768,512]{1,0:T(8,128)(2,1)S(1)}, u32[]{:S(2)}, u32[]{:S(2)}) collective-permute-start(bf16[768,512]{1,0:T(8,128)(2,1)S(1)} %collective-permute-done.19.right_m), channel_id=1, source_target_pairs={{0,12},{1,5},{2,14},{3,7},{4,0},{5,9},{6,2},{7,11},{8,4},{9,13},{1... | collective-permute-start | bytes 2359304 | tf_op jit(solution)/shard_map/ppermute | solution.py:105
  458.0 63.4 %collective-permute-start.11 = (bf16[512,512]{1,0:T(8,128)(2,1)S(1)}, bf16[512,512]{1,0:T(8,128)(2,1)S(1)}, u32[]{:S(2)}, u32[]{:S(2)}) collective-permute-start(bf16[512,512]{1,0:T(8,128)(2,1)S(1)} %copy-done.6), channel_id=1, source_target_pairs={{0,12},{1,5},{2,14},{3,7},{4,0},{5,9},{6,2},{7,11},{8,4},{9,13},{1... | collective-permute-start | bytes 1572872 | tf_op jit(solution)/shard_map/ppermute | solution.py:107
  476.9 46.9 %collective-permute-start.12 = (bf16[512,512]{1,0:T(8,128)(2,1)S(1)}, bf16[512,512]{1,0:T(8,128)(2,1)S(1)}, u32[]{:S(2)}, u32[]{:S(2)}) collective-permute-start(bf16[512,512]{1,0:T(8,128)(2,1)S(1)} %copy-done.4), channel_id=1, source_target_pairs={{0,4},{1,13},{2,6},{3,15},{4,8},{5,1},{6,10},{7,3},{8,12},{9,5},{1... | collective-permute-start | bytes 1572872 | tf_op jit(solution)/shard_map/ppermute | solution.py:106
  478.9 41.0 %copy-start.9 = (bf16[256,512]{1,0:T(8,128)(2,1)S(1)}, bf16[256,512]{1,0:T(8,128)(2,1)}, u32[]{:S(2)}) copy-start(bf16[256,512]{1,0:T(8,128)(2,1)} %copy-done.8) | copy-start | bytes 786436
  478.9 41.0 %collective-permute-start.4 = (bf16[256,512]{1,0:T(8,128)(2,1)S(1)}, bf16[256,512]{1,0:T(8,128)(2,1)S(1)}, u32[]{:S(2)}, u32[]{:S(2)}) collective-permute-start(bf16[256,512]{1,0:T(8,128)(2,1)S(1)} %copy-done.7), channel_id=1, source_target_pairs={{0,12},{1,5},{2,14},{3,7},{4,0},{5,9},{6,2},{7,11},{8,4},{9,13},{1... | collective-permute-start | bytes 786440 | tf_op jit(solution)/shard_map/ppermute | solution.py:94
  479.4 49.9 %collective-permute-start.10 = (bf16[512,512]{1,0:T(8,128)(2,1)S(1)}, bf16[512,512]{1,0:T(8,128)(2,1)S(1)}, u32[]{:S(2)}, u32[]{:S(2)}) collective-permute-start(bf16[512,512]{1,0:T(8,128)(2,1)S(1)} %collective-permute-done.9.left_p), channel_id=1, source_target_pairs={{0,4},{1,13},{2,6},{3,15},{4,8},{5,1},{6,10},{7,3},{8,12},{9,5},{1... | collective-permute-start | bytes 1572872 | tf_op jit(solution)/shard_map/ppermute | solution.py:104
  491.7 45.9 %collective-permute-start.14 = (bf16[512,512]{1,0:T(8,128)(2,1)S(1)}, bf16[512,512]{1,0:T(8,128)(2,1)S(1)}, u32[]{:S(2)}, u32[]{:S(2)}) collective-permute-start(bf16[512,512]{1,0:T(8,128)(2,1)S(1)} %collective-permute-done.13.right_m), channel_id=1, source_target_pairs={{0,12},{1,5},{2,14},{3,7},{4,0},{5,9},{6,2},{7,11},{8,4},{9,13},{1... | collective-permute-start | bytes 1572872 | tf_op jit(solution)/shard_map/ppermute | solution.py:105
  519.9 31.5 %collective-permute-start.2 = (bf16[256,512]{1,0:T(8,128)(2,1)S(1)}, bf16[256,512]{1,0:T(8,128)(2,1)S(1)}, u32[]{:S(2)}, u32[]{:S(2)}) collective-permute-start(bf16[256,512]{1,0:T(8,128)(2,1)S(1)} %copy-done.9), channel_id=1, source_target_pairs={{0,12},{1,5},{2,14},{3,7},{4,0},{5,9},{6,2},{7,11},{8,4},{9,13},{1... | collective-permute-start | bytes 786440 | tf_op jit(solution)/shard_map/ppermute | solution.py:107
  521.4 30.0 %collective-permute-start.3 = (bf16[256,512]{1,0:T(8,128)(2,1)S(1)}, bf16[256,512]{1,0:T(8,128)(2,1)S(1)}, u32[]{:S(2)}, u32[]{:S(2)}) collective-permute-start(bf16[256,512]{1,0:T(8,128)(2,1)S(1)} %copy-done.7), channel_id=1, source_target_pairs={{0,4},{1,13},{2,6},{3,15},{4,8},{5,1},{6,10},{7,3},{8,12},{9,5},{1... | collective-permute-start | bytes 786440 | tf_op jit(solution)/shard_map/ppermute | solution.py:106
  523.7 27.7 %collective-permute-start.1 = (bf16[256,512]{1,0:T(8,128)(2,1)S(1)}, bf16[256,512]{1,0:T(8,128)(2,1)S(1)}, u32[]{:S(2)}, u32[]{:S(2)}) collective-permute-start(bf16[256,512]{1,0:T(8,128)(2,1)S(1)} %collective-permute-done.left_p), channel_id=1, source_target_pairs={{0,4},{1,13},{2,6},{3,15},{4,8},{5,1},{6,10},{7,3},{8,12},{9,5},{1... | collective-permute-start | bytes 786440 | tf_op jit(solution)/shard_map/ppermute | solution.py:104
  529.3 22.1 %collective-permute-start.5 = (bf16[256,512]{1,0:T(8,128)(2,1)S(1)}, bf16[256,512]{1,0:T(8,128)(2,1)S(1)}, u32[]{:S(2)}, u32[]{:S(2)}) collective-permute-start(bf16[256,512]{1,0:T(8,128)(2,1)S(1)} %collective-permute-done.4.right_m), channel_id=1, source_target_pairs={{0,12},{1,5},{2,14},{3,7},{4,0},{5,9},{6,2},{7,11},{8,4},{9,13},{1... | collective-permute-start | bytes 786440 | tf_op jit(solution)/shard_map/ppermute | solution.py:105
